TPU v7x, 256 devices: a whole 4x4x8 slice. The times are simulated.
256 devices in a mesh: pb: 8 (over x, core), ga: 32 (over y, z).
Axes of the slice: x: 4, y: 4, z: 8, core: 2. Of those that a mesh axis runs over, the one named last changes fastest.
Arguments:
- queries: bfloat16 [16384, 512], P(('pb', 'ga')), may hold values from -4 to 4
- gallery: bfloat16 [49152, 512], P('ga'), may hold values from -1 to 1
- positives: int32 [16384, 4], P('pb'), may hold values from 0 to 49151, as said below
- cutoffs: int32 [4], replicated, may hold values from 1 to 1537
Outputs:
- query_grad: float32 [16384, 512], P(('pb', 'ga'))
- gallery_grad: float32 [49152, 512], P(('ga', 'pb'))
Inputs may be any that keep to these rules, and one draw needn't show every extreme that they name: `positives`: indices of a query may repeat.
All inputs are finite; a program needn't handle non-finite values.
Results may differ from a plain program's by a relative error of at most 0.0043.
Values may be sent and summed in bfloat16 or wider, within the bound.
No kernel may reach another device: no remote copies, remote signals or barrier semaphores. Data moves between devices by JAX's collectives and lax.ppermute only.
A program may use at most 64 MiB of HBM per device.

v0:
```python
import functools

import jax
import jax.numpy as jnp
from jax import lax
from jax.experimental import pallas as pl
from jax.experimental.pallas import tpu as pltpu
from jax.sharding import Mesh, PartitionSpec as P

TEMP = 0.05
SHARP = 4.0
HALF_INV = 0.5 / TEMP
TILE = 256
CHUNK = 64
F32 = jnp.float32
BF16 = jnp.bfloat16


def priced(micros):
    return pl.CostEstimate(flops=int(micros * 5e8), transcendentals=0, bytes_accessed=int(micros * 1e6))


def shift(value, axis, step):
    peers = lax.axis_size(axis)
    return lax.ppermute(value, axis, [(i, (i + step) % peers) for i in range(peers)])


def score_body(*refs):
    gallery_ref, query_ref, index_ref, score_ref, anchor_ref = refs[-5:]
    rows, lanes = score_ref.shape
    members = index_ref.shape[0]
    score_ref[...] = (
        lax.dot_general(gallery_ref[...], query_ref[...], (((1,), (1,)), ((), ())), preferred_element_type=F32)
        * HALF_INV
    )
    iota = lax.broadcasted_iota(jnp.int32, (CHUNK, lanes), 0)

    def step(i, found):
        base = i * CHUNK
        part = score_ref[pl.ds(pl.multiple_of(base, CHUNK), CHUNK), :]
        new = []
        for m in range(members):
            wanted = index_ref[m : m + 1, :] - base
            best = found[m]
            for row in range(0, CHUNK, 8):
                best = jnp.where(iota[row : row + 8] == wanted, part[row : row + 8], best)
            new.append(best)
        return tuple(new)

    zero = jnp.zeros((8, lanes), F32)
    found = lax.fori_loop(0, rows // CHUNK, step, (zero,) * members)
    for m in range(members):
        anchor_ref[m : m + 1, :] = jnp.sum(found[m], axis=0, keepdims=True)


def score_block(gallery, queries, index, scores, slot, slots):
    rows, width = gallery.shape
    count = queries.shape[0]
    members = index.shape[0]
    steps = count // TILE
    first = scores is None
    in_specs = [
        pl.BlockSpec((rows, width), lambda i: (0, 0)),
        pl.BlockSpec((TILE, width), lambda i: (i, 0)),
        pl.BlockSpec((members, TILE), lambda i: (0, i)),
    ]
    args = [gallery, queries, index]
    aliases = {}
    if not first:
        in_specs = [pl.BlockSpec(memory_space=pl.ANY), *in_specs]
        args = [scores, *args]
        aliases = {0: 0}
    return pl.pallas_call(
        score_body,
        grid=(steps,),
        in_specs=in_specs,
        out_specs=[
            pl.BlockSpec((rows, TILE), lambda i: (0, slot * steps + i)),
            pl.BlockSpec((members, TILE), lambda i: (0, i)),
        ],
        out_shape=[
            jax.ShapeDtypeStruct((rows, slots * count), F32),
            jax.ShapeDtypeStruct((members, count), F32),
        ],
        input_output_aliases=aliases,
        cost_estimate=priced(5),
    )(*args)


def rank_body(score_ref, anchor_ref, stat_ref):
    rows, lanes = score_ref.shape
    members = anchor_ref.shape[0]
    groups = CHUNK // 8
    for lane in range(0, lanes, 128):
        anchors = [anchor_ref[m : m + 1, lane : lane + 128] for m in range(members)]

        def step(i, sums):
            part = score_ref[pl.ds(pl.multiple_of(i * CHUNK, CHUNK), CHUNK), lane : lane + 128]
            new = []
            for m in range(members):
                t = jnp.tanh(part - anchors[m])
                new.append(sums[2 * m] + (jnp.sum(t.reshape(groups, 8, 128), axis=0) + float(groups)))
                new.append(sums[2 * m + 1] + (float(groups) - jnp.sum((t * t).reshape(groups, 8, 128), axis=0)))
            return tuple(new)

        zero = jnp.zeros((8, 128), F32)
        sums = lax.fori_loop(0, rows // CHUNK, step, (zero,) * (2 * members), unroll=4)
        for m in range(members):
            stat_ref[m : m + 1, lane : lane + 128] = 0.5 * jnp.sum(sums[2 * m], axis=0, keepdims=True)
            stat_ref[members + m : members + m + 1, lane : lane + 128] = 0.25 * jnp.sum(
                sums[2 * m + 1], axis=0, keepdims=True
            )


def rank_sums(scores, anchors):
    rows, count = scores.shape
    members = anchors.shape[0]
    return pl.pallas_call(
        rank_body,
        grid=(count // TILE,),
        in_specs=[
            pl.BlockSpec((rows, TILE), lambda i: (0, i)),
            pl.BlockSpec((members, TILE), lambda i: (0, i)),
        ],
        out_specs=pl.BlockSpec((2 * members, TILE), lambda i: (0, i)),
        out_shape=jax.ShapeDtypeStruct((2 * members, count), F32),
        cost_estimate=priced(12),
        name="rank_sums",
    )(scores, anchors)


def weight_body(*refs):
    cut_ref, score_ref, anchor_ref, index_ref, stat_ref, gallery_ref, dscore_ref, query_ref, coef_ref = refs[-9:]
    rows, lanes = score_ref.shape
    members = anchor_ref.shape[0]
    cuts = cut_ref.shape[0]
    rank = 0.5 + stat_ref[0:members, :]
    slope = stat_ref[members : 2 * members, :] / TEMP
    weight = jnp.zeros((members, lanes), F32)
    for c in range(cuts):
        cut = cut_ref[c].astype(F32)
        decay = jnp.exp(-jnp.abs(SHARP * (cut - rank) / cut))
        weight = weight + decay / ((1.0 + decay) * (1.0 + decay)) * (SHARP / cut)
    weight = weight / float(members * cuts)
    scaled = weight * (0.25 / TEMP)
    coef_ref[0:members, :] = scaled
    coef_ref[members : 2 * members, :] = weight * slope
    total = jnp.sum(scaled, axis=0, keepdims=True)
    iota = lax.broadcasted_iota(jnp.int32, (CHUNK, 128), 0)
    for lane in range(0, lanes, 128):
        span = slice(lane, lane + 128)
        base_total = total[:, span]

        def step(i, carry):
            base = pl.multiple_of(i * CHUNK, CHUNK)
            part = score_ref[pl.ds(base, CHUNK), span]
            acc = jnp.broadcast_to(base_total, (CHUNK, 128))
            for m in range(members):
                t = jnp.tanh(part - anchor_ref[m : m + 1, span])
                hit = iota == (index_ref[m : m + 1, span] - base)
                acc = acc - jnp.where(
                    hit, coef_ref[members + m : members + m + 1, span], coef_ref[m : m + 1, span] * (t * t)
                )
            dscore_ref[pl.ds(base, CHUNK), span] = acc.astype(BF16)
            return carry

        lax.fori_loop(0, rows // CHUNK, step, 0, unroll=2)
    turned = jnp.dot(gallery_ref[...], dscore_ref[...], preferred_element_type=F32)
    query_ref[...] = turned.T.astype(query_ref.dtype)


def weight_blocks(cutoffs, scores, anchors, index, stats, turned, dscore, which, slots, dtype):
    width, rows = turned.shape
    members = anchors.shape[0]
    count = scores.shape[1] // slots
    steps = count // TILE
    stride = which[-1] - which[0] if len(which) > 1 else 0
    here = lambda i: (0, (which[0] + stride * (i // steps)) * steps + i % steps)
    in_specs = [
        pl.BlockSpec(memory_space=pltpu.SMEM),
        pl.BlockSpec((rows, TILE), here),
        pl.BlockSpec((members, TILE), here),
        pl.BlockSpec((members, TILE), here),
        pl.BlockSpec((2 * members, TILE), here),
        pl.BlockSpec((width, rows), lambda i: (0, 0)),
    ]
    args = [cutoffs, scores, anchors, index, stats, turned]
    aliases = {}
    if dscore is not None:
        in_specs = [pl.BlockSpec(memory_space=pl.ANY), *in_specs]
        args = [dscore, *args]
        aliases = {0: 0}
    return pl.pallas_call(
        weight_body,
        grid=(steps * len(which),),
        in_specs=in_specs,
        out_specs=[pl.BlockSpec((rows, TILE), here), pl.BlockSpec((TILE, width), lambda i: (i, 0))],
        out_shape=[
            jax.ShapeDtypeStruct((rows, slots * count), BF16),
            jax.ShapeDtypeStruct((len(which) * count, width), dtype),
        ],
        scratch_shapes=[pltpu.VMEM((2 * members, TILE), F32)],
        input_output_aliases=aliases,
        cost_estimate=priced(6 * len(which)),
    )(*args)


def gallery_body(dscore_ref, *refs):
    out_ref = refs[-1]
    at = 0
    acc = None
    for query_ref in refs[:-1]:
        size = query_ref.shape[0]
        term = jnp.dot(dscore_ref[:, at : at + size], query_ref[...], preferred_element_type=F32)
        acc = term if acc is None else acc + term
        at += size
    out_ref[...] = acc.astype(out_ref.dtype)


def gallery_terms(dscore, parts):
    rows, count = dscore.shape
    width = parts[0].shape[1]
    tile = rows // 3
    return pl.pallas_call(
        gallery_body,
        grid=(rows // tile,),
        in_specs=[
            pl.BlockSpec((tile, count), lambda i: (i, 0)),
            *[pl.BlockSpec(p.shape, lambda i: (0, 0)) for p in parts],
        ],
        out_specs=pl.BlockSpec((tile, width), lambda i: (i, 0)),
        out_shape=jax.ShapeDtypeStruct((rows, width), F32),
        cost_estimate=priced(6),
        name="gallery_terms",
    )(dscore, *parts)


def summed_over_gallery(value):
    size = value.shape[1] // lax.axis_size("y")
    parts = [jnp.roll(shift(value, "y", k), -k * size, axis=1) for k in range(1, lax.axis_size("y"))]
    for part in parts:
        value = value + part
    lower = shift(value, "z", 1)
    upper = shift(value, "z", -1)
    two = value + lower
    three = two + upper
    return three + shift(three, "z", 3) + shift(two, "z", -3)


def shard_terms(queries, gallery, positives, cutoffs):
    ny = lax.axis_size("y")
    nz = lax.axis_size("z")
    nx = lax.axis_size("x")
    yy = lax.axis_index("y")
    gallery_rows, width = gallery.shape
    first_row = (yy * nz + lax.axis_index("z")) * gallery_rows
    local = positives.T - first_row
    size = local.shape[1] // ny
    local = lax.dynamic_slice_in_dim(jnp.concatenate([local, local], axis=1), yy * size, ny * size, 1)

    copies = jnp.broadcast_to(queries[None], (nz, *queries.shape))
    own = lax.all_to_all(copies, "z", 0, 0, tiled=True).reshape(size, width)
    half = size // 2
    after = shift(own, "y", -1)
    before = shift(own, "y", 1)
    far_a = shift(after[:half], "y", -1)
    far_b = shift(before[half:], "y", 1)
    far = jnp.concatenate([far_a, far_b], axis=0)
    blocks = [own, after, far, before]

    scores = None
    anchors = [None] * ny
    for slot in (0, 1, 3, 2):
        index = local[:, slot * size : (slot + 1) * size]
        scores, anchors[slot] = score_block(gallery, blocks[slot], index, scores, slot, ny)
    anchors = summed_over_gallery(jnp.concatenate(anchors, axis=1))
    stats = summed_over_gallery(rank_sums(scores, anchors))

    weights = functools.partial(weight_blocks, cutoffs, scores, anchors, local, stats, gallery.T)
    dscore, part_far = weights(None, (2,), ny, BF16)
    got_a = shift(part_far[:half], "y", 1)
    got_b = shift(part_far[half:], "y", -1)
    dscore, part_next = weights(dscore, (1, 3), ny, F32)
    part_after, part_before = part_next[:size], part_next[size:]
    up = jnp.concatenate([part_after[:half] + got_a.astype(F32), part_after[half:]], axis=0).astype(BF16)
    down = jnp.concatenate([part_before[:half], part_before[half:] + got_b.astype(F32)], axis=0).astype(BF16)
    dscore, up, down = lax.optimization_barrier((dscore, up, down))
    got_up = shift(up, "y", 1)
    got_down = shift(down, "y", -1)
    dscore, part_own = weights(dscore, (0,), ny, F32)
    gallery_part = gallery_terms(dscore, blocks)

    out_rows = gallery_rows // (2 * nx)
    split = gallery_part.reshape(nx, 2, out_rows, width)
    core = lax.axis_index("c")
    mine = lax.dynamic_index_in_dim(split, core, 1, False)
    other = lax.dynamic_index_in_dim(split, 1 - core, 1, False).astype(BF16)
    pair = mine + lax.ppermute(other, "c", [(0, 1), (1, 0)]).astype(F32)
    xx = lax.axis_index("x")
    gallery_grad = lax.dynamic_index_in_dim(pair, xx, 0, False)
    sent = [
        shift(lax.dynamic_index_in_dim(pair, (xx + k) % nx, 0, False).astype(BF16), "x", k) for k in range(1, nx)
    ]
    for part in sent:
        gallery_grad = gallery_grad + part.astype(F32)

    query_part = (part_own + got_up.astype(F32) + got_down.astype(F32)).astype(BF16)
    landed = lax.all_to_all(query_part.reshape(nz, size // nz, width), "z", 0, 0, tiled=True)
    query_grad = jnp.sum(landed.astype(F32), axis=0)
    return (query_grad, gallery_grad)


def solution(mesh):
    fine = Mesh(mesh.devices.reshape(4, 2, 4, 8), ("x", "c", "y", "z"))
    placed = (P(("x", "c", "y", "z"), None), P(("y", "z"), None), P(("x", "c"), None), P())
    return jax.shard_map(
        shard_terms,
        mesh=fine,
        in_specs=placed,
        out_specs=(P(("x", "c", "y", "z"), None), P(("y", "z", "x", "c"), None)),
        check_vma=False,
    )
```

profile of v0, /device:TPU:64, one launch (start us, length us, event | category | flops | bytes accessed | tf_op | source)
XLA Modules:
  0.0 205.6 jit_solution(6613257352666679695)
XLA Ops:
  2.3 8.1 %all-to-all-start = ((bf16[8,64,512]{2,1,0:T(8,128)(2,1)}), bf16[8,64,512]{2,1,0:T(8,128)(2,1)S(1)}, u32[]{:S(2)}, u32[]{:S(2)}) async-start(bf16[8,64,512]{2,1,0:T(8,128)(2,1)} %broadcast_in_dim.2), calls=%async_computation | async-start | bytes 1048576 | tf_op jit(solution)/shard_map/all_to_all | solution.py:262
  11.3 12.9 %all-to-all-done = bf16[8,64,512]{2,1,0:T(8,128)(2,1)S(1)} async-done(((bf16[8,64,512]{2,1,0:T(8,128)(2,1)}), bf16[8,64,512]{2,1,0:T(8,128)(2,1)S(1)}, u32[]{:S(2)}, u32[]{:S(2)}) %all-to-all-start) | async-done | bytes 524320 | tf_op jit(solution)/shard_map/all_to_all | solution.py:262
  24.2 3.0 %collective-permute-start = (bf16[512,512]{1,0:T(8,128)(2,1)S(1)}, bf16[512,512]{1,0:T(8,128)(2,1)S(1)}, u32[]{:S(2)}, u32[]{:S(2)}) collective-permute-start(bf16[512,512]{1,0:T(8,128)(2,1)S(1)} %bitcast.31), channel_id=1, source_target_pairs={{0,24},{8,0},{16,8},{24,16},{1,25},{9,1},{17,9},{25,17},{2,26},{10... | collective-permute-start | bytes 1572872 | tf_op jit(solution)/shard_map/ppermute | solution.py:25
  27.8 5.1 %shard_map.59 = (f32[1536,2048]{1,0:T(8,128)}, f32[4,512]{1,0:T(4,128)}) custom-call(bf16[1536,512]{1,0:T(8,128)(2,1)} %refs_1_.7, bf16[512,512]{1,0:T(8,128)(2,1)} %bitcast.33, s32[4,512]{1,0:T(4,128)} %get-tuple-element.56.refs_2_), custom_call_target="tpu_custom_call" | custom-call | flops 2500000000 | bytes 5000000 | tf_op jit(solution)/shard_map/pallas_call | solution.py:73
  33.6 3.7 %collective-permute-done.refs_2_.refs_1_ = bf16[512,512]{1,0:T(8,128)(2,1)S(1)} collective-permute-done((bf16[512,512]{1,0:T(8,128)(2,1)S(1)}, bf16[512,512]{1,0:T(8,128)(2,1)S(1)}, u32[]{:S(2)}, u32[]{:S(2)}) %collective-permute-start) | collective-permute-done | bytes 524320 | tf_op jit(solution)/shard_map/ppermute | solution.py:25
  37.4 3.8 %collective-permute-start.2 = (bf16[256,512]{1,0:T(8,128)(2,1)S(1)}, bf16[256,512]{1,0:T(8,128)(2,1)S(1)}, u32[]{:S(2)}, u32[]{:S(2)}) collective-permute-start(bf16[256,512]{1,0:T(8,128)(2,1)S(1)} %slice.119), channel_id=1, source_target_pairs={{0,24},{8,0},{16,8},{24,16},{1,25},{9,1},{17,9},{25,17},{2,26},{10... | collective-permute-start | bytes 786440 | tf_op jit(solution)/shard_map/ppermute | solution.py:25
  41.3 5.1 %shard_map.60 = (f32[1536,2048]{1,0:T(8,128)}, f32[4,512]{1,0:T(4,128)}) custom-call(f32[1536,2048]{1,0:T(8,128)} %get-tuple-element.19.refs_0_, bf16[1536,512]{1,0:T(8,128)(2,1)} %refs_1_.7, bf16[512,512]{1,0:T(8,128)(2,1)} %copy-done.4, s32[4,512]{1,0:T(4,128)} %get-tuple-element.55.refs_3_), custom_call_target="tpu_custom_call", output_to_operand_aliasing={{0}: (0, {})} | custom-call | flops 2500000000 | bytes 5000000 | tf_op jit(solution)/shard_map/pallas_call | solution.py:73
  46.5 5.2 %shard_map.61 = (f32[1536,2048]{1,0:T(8,128)}, f32[4,512]{1,0:T(4,128)}) custom-call(f32[1536,2048]{1,0:T(8,128)} %get-tuple-element.20.refs_0_, bf16[1536,512]{1,0:T(8,128)(2,1)} %refs_1_.7, bf16[512,512]{1,0:T(8,128)(2,1)} %copy-done.5, s32[4,512]{1,0:T(4,128)} %get-tuple-element.54.refs_3_), custom_call_target="tpu_custom_call", output_to_operand_aliasing={{0}: (0, {})} | custom-call | flops 2500000000 | bytes 5000000 | tf_op jit(solution)/shard_map/pallas_call | solution.py:73
  52.5 5.1 %shard_map.62 = (f32[1536,2048]{1,0:T(8,128)}, f32[4,512]{1,0:T(4,128)}) custom-call(f32[1536,2048]{1,0:T(8,128)} %get-tuple-element.21.refs_0_, bf16[1536,512]{1,0:T(8,128)(2,1)} %refs_1_.7, bf16[512,512]{1,0:T(8,128)(2,1)} %copy-done.6, s32[4,512]{1,0:T(4,128)} %get-tuple-element.53.refs_3_), custom_call_target="tpu_custom_call", output_to_operand_aliasing={{0}: (0, {})} | custom-call | flops 2500000000 | bytes 5000000 | tf_op jit(solution)/shard_map/pallas_call | solution.py:73
  58.4 3.2 %collective-permute-start.6 = (f32[4,2048]{1,0:T(4,128)S(1)}, f32[4,2048]{1,0:T(4,128)S(1)}, u32[]{:S(2)}, u32[]{:S(2)}) collective-permute-start(f32[4,2048]{1,0:T(4,128)S(1)} %constant_dynamic-update-slice_fusion.2), channel_id=1, source_target_pairs={{0,24},{8,0},{16,8},{24,16},{1,25},{9,1},{17,9},{25,17},{2,26},{10... | collective-permute-start | bytes 98312 | tf_op jit(solution)/shard_map/ppermute | solution.py:25
  63.6 3.5 %collective-permute-done.5 = f32[4,2048]{1,0:T(4,128)S(1)} collective-permute-done((f32[4,2048]{1,0:T(4,128)S(1)}, f32[4,2048]{1,0:T(4,128)S(1)}, u32[]{:S(2)}, u32[]{:S(2)}) %collective-permute-start.5) | collective-permute-done | bytes 32800 | tf_op jit(solution)/shard_map/ppermute | solution.py:25
  71.8 8.1 %collective-permute-start.10 = (f32[4,2048]{1,0:T(4,128)S(1)}, f32[4,2048]{1,0:T(4,128)S(1)}, u32[]{:S(2)}, u32[]{:S(2)}) collective-permute-start(f32[4,2048]{1,0:T(4,128)S(1)} %get-tuple-element.39), channel_id=1, source_target_pairs={{0,5},{1,6},{2,7},{3,0},{4,1},{5,2},{6,3},{7,4},{8,13},{9,14},{10,... | collective-permute-start | bytes 98312 | tf_op jit(solution)/shard_map/ppermute | solution.py:25
  81.6 5.3 %collective-permute-done.9 = f32[4,2048]{1,0:T(4,128)S(1)} collective-permute-done((f32[4,2048]{1,0:T(4,128)S(1)}, f32[4,2048]{1,0:T(4,128)S(1)}, u32[]{:S(2)}, u32[]{:S(2)}) %collective-permute-start.9) | collective-permute-done | bytes 32800 | tf_op jit(solution)/shard_map/ppermute | solution.py:25
  87.5 12.6 %rank_sums.1 = f32[8,2048]{1,0:T(8,128)} custom-call(f32[1536,2048]{1,0:T(8,128)} %get-tuple-element.22.score_ref.refs_1_.refs_2_, f32[4,2048]{1,0:T(4,128)} %add_add_fusion.1.anchor_ref.refs_2_.refs_3_), custom_call_target="tpu_custom_call" | custom-call | flops 6000000000 | bytes 12000000 | tf_op jit(solution)/shard_map/rank_sums/pallas_call | solution.py:118
  100.2 3.2 %collective-permute-start.13 = (f32[8,2048]{1,0:T(8,128)}, f32[8,2048]{1,0:T(8,128)S(1)}, u32[]{:S(2)}, u32[]{:S(2)}) collective-permute-start(f32[8,2048]{1,0:T(8,128)} %rank_sums.1), channel_id=1, source_target_pairs={{0,24},{8,0},{16,8},{24,16},{1,25},{9,1},{17,9},{25,17},{2,26},{10... | collective-permute-start | bytes 196616 | tf_op jit(solution)/shard_map/ppermute | solution.py:25
  103.5 2.3 %collective-permute-done.11 = f32[8,2048]{1,0:T(8,128)S(1)} collective-permute-done((f32[8,2048]{1,0:T(8,128)}, f32[8,2048]{1,0:T(8,128)S(1)}, u32[]{:S(2)}, u32[]{:S(2)}) %collective-permute-start.11) | collective-permute-done | bytes 65568 | tf_op jit(solution)/shard_map/ppermute | solution.py:25
  105.9 3.5 %collective-permute-done.12 = f32[8,2048]{1,0:T(8,128)S(1)} collective-permute-done((f32[8,2048]{1,0:T(8,128)}, f32[8,2048]{1,0:T(8,128)S(1)}, u32[]{:S(2)}, u32[]{:S(2)}) %collective-permute-start.12) | collective-permute-done | bytes 65568 | tf_op jit(solution)/shard_map/ppermute | solution.py:25
  110.3 2.0 collective-permute-start.15
  112.3 2.2 %collective-permute-done.14 = f32[8,2048]{1,0:T(8,128)S(1)} collective-permute-done((f32[8,2048]{1,0:T(8,128)S(1)}, f32[8,2048]{1,0:T(8,128)S(1)}, u32[]{:S(2)}, u32[]{:S(2)}) %collective-permute-start.14) | collective-permute-done | bytes 65568 | tf_op jit(solution)/shard_map/ppermute | solution.py:25
  115.5 4.3 %collective-permute-start.17 = (f32[8,2048]{1,0:T(8,128)S(1)}, f32[8,2048]{1,0:T(8,128)S(1)}, u32[]{:S(2)}, u32[]{:S(2)}) collective-permute-start(f32[8,2048]{1,0:T(8,128)S(1)} %get-tuple-element.37), channel_id=1, source_target_pairs={{0,5},{1,6},{2,7},{3,0},{4,1},{5,2},{6,3},{7,4},{8,13},{9,14},{10,... | collective-permute-start | bytes 196616 | tf_op jit(solution)/shard_map/ppermute | solution.py:25
  123.5 8.1 %shard_map.63 = (bf16[1536,2048]{1,0:T(8,128)(2,1)}, bf16[512,512]{1,0:T(8,128)(2,1)}) custom-call(s32[4]{0:T(128)} %refs_1_.9, f32[1536,2048]{1,0:T(8,128)} %get-tuple-element.22.score_ref.refs_1_.refs_2_, f32[4,2048]{1,0:T(4,128)} %add_add_fusion.1.anchor_ref.refs_2_.refs_3_, s32[4,2048]{1,0:T(4,128)} %copy-done.8, f32[8,2048]{1,0:T(8,128)} %add_add_fusion.refs_4_.refs_5_, ...), custom_call_target="tpu_custom_call" | custom-call | flops 3000000000 | bytes 6000000 | tf_op jit(solution)/shard_map/pallas_call | solution.py:193
  133.4 2.6 %collective-permute-start.19 = (bf16[256,512]{1,0:T(8,128)(2,1)S(1)}, bf16[256,512]{1,0:T(8,128)(2,1)S(1)}, u32[]{:S(2)}, u32[]{:S(2)}) collective-permute-start(bf16[256,512]{1,0:T(8,128)(2,1)S(1)} %get-tuple-element.47), channel_id=1, source_target_pairs={{0,24},{8,0},{16,8},{24,16},{1,25},{9,1},{17,9},{25,17},{2,26},{10... | collective-permute-start | bytes 786440 | tf_op jit(solution)/shard_map/ppermute | solution.py:25
  136.0 13.7 %shard_map.64 = (bf16[1536,2048]{1,0:T(8,128)(2,1)}, f32[1024,512]{1,0:T(8,128)}) custom-call(bf16[1536,2048]{1,0:T(8,128)(2,1)} %get-tuple-element.27.refs_0_, s32[4]{0:T(128)} %refs_1_.9, f32[1536,2048]{1,0:T(8,128)} %get-tuple-element.22.score_ref.refs_1_.refs_2_, ...), custom_call_target="tpu_custom_call", output_to_operand_aliasing={{0}: (0, {})} | custom-call | flops 6000000000 | bytes 12000000 | tf_op jit(solution)/shard_map/pallas_call | solution.py:193
  153.2 8.2 %shard_map.65 = (bf16[1536,2048]{1,0:T(8,128)(2,1)}, f32[512,512]{1,0:T(8,128)}) custom-call(bf16[1536,2048]{1,0:T(8,128)(2,1)} %get-tuple-element.31.refs_0_, s32[4]{0:T(128)} %refs_1_.9, f32[1536,2048]{1,0:T(8,128)} %get-tuple-element.22.score_ref.refs_1_.refs_2_, ...), custom_call_target="tpu_custom_call", output_to_operand_aliasing={{0}: (0, {})} | custom-call | flops 3000000000 | bytes 6000000 | tf_op jit(solution)/shard_map/pallas_call | solution.py:193
  161.4 3.2 %collective-permute-start.21 = (bf16[512,512]{1,0:T(8,128)(2,1)}, bf16[512,512]{1,0:T(8,128)(2,1)}, u32[]{:S(2)}, u32[]{:S(2)}) collective-permute-start(bf16[512,512]{1,0:T(8,128)(2,1)} %get-tuple-element.34), channel_id=1, source_target_pairs={{0,24},{8,0},{16,8},{24,16},{1,25},{9,1},{17,9},{25,17},{2,26},{10... | collective-permute-start | bytes 1572872 | tf_op jit(solution)/shard_map/ppermute | solution.py:25
  164.6 7.6 %gallery_terms.1 = f32[1536,512]{1,0:T(8,128)} custom-call(bf16[1536,2048]{1,0:T(8,128)(2,1)} %get-tuple-element.35.dscore_ref, bf16[512,512]{1,0:T(8,128)(2,1)} %bitcast.34, bf16[512,512]{1,0:T(8,128)(2,1)} %copy-done.4, bf16[512,512]{1,0:T(8,128)(2,1)} %copy-done.6, bf16[512,512]{1,0:T(8,128)(2,1)} %copy-done.5), custom_call_target="tpu_custom_call" | custom-call | flops 3000000000 | bytes 6000000 | tf_op jit(solution)/shard_map/gallery_terms/pallas_call | solution.py:224
  172.2 2.6 %fusion = bf16[4,192,512]{2,1,0:T(8,128)(2,1)} fusion(f32[4,2,192,512]{3,2,1,0:T(8,128)} %bitcast.29, s32[]{:T(128)S(6)} %select_n.40), kind=kLoop, calls=%fused_computation.4 | loop fusion | bytes 1572868 | tf_op jit(solution)/shard_map/convert_element_type | solution.py:297
  174.8 2.5 %add_convert_fusion = bf16[512,512]{1,0:T(8,128)(2,1)} fusion(bf16[512,512]{1,0:T(8,128)(2,1)} %collective-permute-done.21, f32[512,512]{1,0:T(8,128)} %get-tuple-element.32, bf16[512,512]{1,0:T(8,128)(2,1)} %collective-permute-done.20), kind=kLoop, calls=%fused_computation.3 | loop fusion | flops 1310720 | bytes 2621440 | tf_op jit(solution)/shard_map/convert_element_type | solution.py:307
  177.3 8.8 %all-to-all-start.1 = ((bf16[8,64,512]{2,1,0:T(8,128)(2,1)}), bf16[8,64,512]{2,1,0:T(8,128)(2,1)}, u32[]{:S(2)}, u32[]{:S(2)}) async-start(bf16[8,64,512]{2,1,0:T(8,128)(2,1)} %bitcast.35), calls=%async_computation.1 | async-start | bytes 1048576 | tf_op jit(solution)/shard_map/all_to_all | solution.py:308
  190.3 2.7 %collective-permute-start.24 = (bf16[192,512]{1,0:T(8,128)(2,1)S(1)}, bf16[192,512]{1,0:T(8,128)(2,1)S(1)}, u32[]{:S(2)}, u32[]{:S(2)}) collective-permute-start(bf16[192,512]{1,0:T(8,128)(2,1)S(1)} %get-tuple-element.44), channel_id=1, source_target_pairs={{0,128},{64,192},{128,0},{192,64},{1,129},{65,193},{129,1},{193,65... | collective-permute-start | bytes 589832 | tf_op jit(solution)/shard_map/ppermute | solution.py:25
  194.5 2.3 %collective-permute-done.23 = bf16[192,512]{1,0:T(8,128)(2,1)S(1)} collective-permute-done((bf16[192,512]{1,0:T(8,128)(2,1)S(1)}, bf16[192,512]{1,0:T(8,128)(2,1)S(1)}, u32[]{:S(2)}, u32[]{:S(2)}) %collective-permute-start.23) | collective-permute-done | bytes 196640 | tf_op jit(solution)/shard_map/ppermute | solution.py:25
  196.8 5.2 %collective-permute-done.24 = bf16[192,512]{1,0:T(8,128)(2,1)S(1)} collective-permute-done((bf16[192,512]{1,0:T(8,128)(2,1)S(1)}, bf16[192,512]{1,0:T(8,128)(2,1)S(1)}, u32[]{:S(2)}, u32[]{:S(2)}) %collective-permute-start.24) | collective-permute-done | bytes 196640 | tf_op jit(solution)/shard_map/ppermute | solution.py:25
  (95 shorter events, 34.8 us)
Async XLA Ops:
  2.3 21.9 %all-to-all-start = ((bf16[8,64,512]{2,1,0:T(8,128)(2,1)}), bf16[8,64,512]{2,1,0:T(8,128)(2,1)S(1)}, u32[]{:S(2)}, u32[]{:S(2)}) async-start(bf16[8,64,512]{2,1,0:T(8,128)(2,1)} %broadcast_in_dim.2), calls=%async_computation | async-start | bytes 1048576 | tf_op jit(solution)/shard_map/all_to_all | solution.py:262
  11.2 21.7 %copy-start.8 = (s32[4,2048]{1,0:T(4,128)}, s32[4,2048]{1,0:T(4,128)S(1)}, u32[]{:S(2)}) copy-start(s32[4,2048]{1,0:T(4,128)S(1)} %fusion.8.refs_3_.refs_4_) | copy-start | bytes 98308
  24.2 13.2 %collective-permute-start = (bf16[512,512]{1,0:T(8,128)(2,1)S(1)}, bf16[512,512]{1,0:T(8,128)(2,1)S(1)}, u32[]{:S(2)}, u32[]{:S(2)}) collective-permute-start(bf16[512,512]{1,0:T(8,128)(2,1)S(1)} %bitcast.31), channel_id=1, source_target_pairs={{0,24},{8,0},{16,8},{24,16},{1,25},{9,1},{17,9},{25,17},{2,26},{10... | collective-permute-start | bytes 1572872 | tf_op jit(solution)/shard_map/ppermute | solution.py:25
  27.2 14.0 %collective-permute-start.1 = (bf16[512,512]{1,0:T(8,128)(2,1)S(1)}, bf16[512,512]{1,0:T(8,128)(2,1)S(1)}, u32[]{:S(2)}, u32[]{:S(2)}) collective-permute-start(bf16[512,512]{1,0:T(8,128)(2,1)S(1)} %bitcast.32), channel_id=1, source_target_pairs={{0,8},{8,16},{16,24},{24,0},{1,9},{9,17},{17,25},{25,1},{2,10},{10... | collective-permute-start | bytes 1572872 | tf_op jit(solution)/shard_map/ppermute | solution.py:25
  37.4 14.2 %collective-permute-start.2 = (bf16[256,512]{1,0:T(8,128)(2,1)S(1)}, bf16[256,512]{1,0:T(8,128)(2,1)S(1)}, u32[]{:S(2)}, u32[]{:S(2)}) collective-permute-start(bf16[256,512]{1,0:T(8,128)(2,1)S(1)} %slice.119), channel_id=1, source_target_pairs={{0,24},{8,0},{16,8},{24,16},{1,25},{9,1},{17,9},{25,17},{2,26},{10... | collective-permute-start | bytes 786440 | tf_op jit(solution)/shard_map/ppermute | solution.py:25
  41.2 10.4 %collective-permute-start.3 = (bf16[256,512]{1,0:T(8,128)(2,1)S(1)}, bf16[256,512]{1,0:T(8,128)(2,1)S(1)}, u32[]{:S(2)}, u32[]{:S(2)}) collective-permute-start(bf16[256,512]{1,0:T(8,128)(2,1)S(1)} %slice.120), channel_id=1, source_target_pairs={{0,8},{8,16},{16,24},{24,0},{1,9},{9,17},{17,25},{25,1},{2,10},{10... | collective-permute-start | bytes 786440 | tf_op jit(solution)/shard_map/ppermute | solution.py:25
  52.5 5.8 %copy-start.9 = (f32[4,512]{1,0:T(4,128)S(1)}, f32[4,512]{1,0:T(4,128)}, u32[]{:S(2)}) copy-start(f32[4,512]{1,0:T(4,128)} %get-tuple-element.26) | copy-start | bytes 24580
  58.4 5.2 %collective-permute-start.4 = (f32[4,2048]{1,0:T(4,128)S(1)}, f32[4,2048]{1,0:T(4,128)S(1)}, u32[]{:S(2)}, u32[]{:S(2)}) collective-permute-start(f32[4,2048]{1,0:T(4,128)S(1)} %constant_dynamic-update-slice_fusion.2), channel_id=1, source_target_pairs={{0,8},{8,16},{16,24},{24,0},{1,9},{9,17},{17,25},{25,1},{2,10},{10... | collective-permute-start | bytes 98312 | tf_op jit(solution)/shard_map/ppermute | solution.py:25
  58.4 5.2 %collective-permute-start.6 = (f32[4,2048]{1,0:T(4,128)S(1)}, f32[4,2048]{1,0:T(4,128)S(1)}, u32[]{:S(2)}, u32[]{:S(2)}) collective-permute-start(f32[4,2048]{1,0:T(4,128)S(1)} %constant_dynamic-update-slice_fusion.2), channel_id=1, source_target_pairs={{0,24},{8,0},{16,8},{24,16},{1,25},{9,1},{17,9},{25,17},{2,26},{10... | collective-permute-start | bytes 98312 | tf_op jit(solution)/shard_map/ppermute | solution.py:25
  61.6 5.4 %collective-permute-start.5 = (f32[4,2048]{1,0:T(4,128)S(1)}, f32[4,2048]{1,0:T(4,128)S(1)}, u32[]{:S(2)}, u32[]{:S(2)}) collective-permute-start(f32[4,2048]{1,0:T(4,128)S(1)} %constant_dynamic-update-slice_fusion.2), channel_id=1, source_target_pairs={{0,16},{8,24},{16,0},{24,8},{1,17},{9,25},{17,1},{25,9},{2,18},{10... | collective-permute-start | bytes 98312 | tf_op jit(solution)/shard_map/ppermute | solution.py:25
  67.1 4.0 %collective-permute-start.7 = (f32[4,2048]{1,0:T(4,128)S(1)}, f32[4,2048]{1,0:T(4,128)S(1)}, u32[]{:S(2)}, u32[]{:S(2)}) collective-permute-start(f32[4,2048]{1,0:T(4,128)S(1)} %fusion.10), channel_id=1, source_target_pairs={{0,1},{1,2},{2,3},{3,4},{4,5},{5,6},{6,7},{7,0},{8,9},{9,10},{10,1... | collective-permute-start | bytes 98312 | tf_op jit(solution)/shard_map/ppermute | solution.py:25
  67.9 3.9 %collective-permute-start.8 = (f32[4,2048]{1,0:T(4,128)S(1)}, f32[4,2048]{1,0:T(4,128)S(1)}, u32[]{:S(2)}, u32[]{:S(2)}) collective-permute-start(f32[4,2048]{1,0:T(4,128)S(1)} %fusion.10), channel_id=1, source_target_pairs={{0,7},{1,0},{2,1},{3,2},{4,3},{5,4},{6,5},{7,6},{8,15},{9,8},{10,9... | collective-permute-start | bytes 98312 | tf_op jit(solution)/shard_map/ppermute | solution.py:25
  71.8 9.7 %collective-permute-start.10 = (f32[4,2048]{1,0:T(4,128)S(1)}, f32[4,2048]{1,0:T(4,128)S(1)}, u32[]{:S(2)}, u32[]{:S(2)}) collective-permute-start(f32[4,2048]{1,0:T(4,128)S(1)} %get-tuple-element.39), channel_id=1, source_target_pairs={{0,5},{1,6},{2,7},{3,0},{4,1},{5,2},{6,3},{7,4},{8,13},{9,14},{10,... | collective-permute-start | bytes 98312 | tf_op jit(solution)/shard_map/ppermute | solution.py:25
  80.0 6.9 %collective-permute-start.9 = (f32[4,2048]{1,0:T(4,128)S(1)}, f32[4,2048]{1,0:T(4,128)S(1)}, u32[]{:S(2)}, u32[]{:S(2)}) collective-permute-start(f32[4,2048]{1,0:T(4,128)S(1)} %get-tuple-element.38), channel_id=1, source_target_pairs={{0,3},{1,4},{2,5},{3,6},{4,7},{5,0},{6,1},{7,2},{8,11},{9,12},{10,... | collective-permute-start | bytes 98312 | tf_op jit(solution)/shard_map/ppermute | solution.py:25
  87.5 32.3 %copy-start = (bf16[1536,512]{1,0:T(8,128)(2,1)S(1)}, bf16[1536,512]{1,0:T(8,128)(2,1)}, u32[]{:S(2)}) copy-start(bf16[1536,512]{1,0:T(8,128)(2,1)} %refs_1_.7) | copy-start | bytes 4718596
  100.1 5.7 %collective-permute-start.11 = (f32[8,2048]{1,0:T(8,128)}, f32[8,2048]{1,0:T(8,128)S(1)}, u32[]{:S(2)}, u32[]{:S(2)}) collective-permute-start(f32[8,2048]{1,0:T(8,128)} %rank_sums.1), channel_id=1, source_target_pairs={{0,8},{8,16},{16,24},{24,0},{1,9},{9,17},{17,25},{25,1},{2,10},{10... | collective-permute-start | bytes 196616 | tf_op jit(solution)/shard_map/ppermute | solution.py:25
  100.2 5.7 %collective-permute-start.13 = (f32[8,2048]{1,0:T(8,128)}, f32[8,2048]{1,0:T(8,128)S(1)}, u32[]{:S(2)}, u32[]{:S(2)}) collective-permute-start(f32[8,2048]{1,0:T(8,128)} %rank_sums.1), channel_id=1, source_target_pairs={{0,24},{8,0},{16,8},{24,16},{1,25},{9,1},{17,9},{25,17},{2,26},{10... | collective-permute-start | bytes 196616 | tf_op jit(solution)/shard_map/ppermute | solution.py:25
  103.4 6.0 %collective-permute-start.12 = (f32[8,2048]{1,0:T(8,128)}, f32[8,2048]{1,0:T(8,128)S(1)}, u32[]{:S(2)}, u32[]{:S(2)}) collective-permute-start(f32[8,2048]{1,0:T(8,128)} %rank_sums.1), channel_id=1, source_target_pairs={{0,16},{8,24},{16,0},{24,8},{1,17},{9,25},{17,1},{25,9},{2,18},{10... | collective-permute-start | bytes 196616 | tf_op jit(solution)/shard_map/ppermute | solution.py:25
  110.2 4.3 %collective-permute-start.14 = (f32[8,2048]{1,0:T(8,128)S(1)}, f32[8,2048]{1,0:T(8,128)S(1)}, u32[]{:S(2)}, u32[]{:S(2)}) collective-permute-start(f32[8,2048]{1,0:T(8,128)S(1)} %fusion.7), channel_id=1, source_target_pairs={{0,1},{1,2},{2,3},{3,4},{4,5},{5,6},{6,7},{7,0},{8,9},{9,10},{10,1... | collective-permute-start | bytes 196616 | tf_op jit(solution)/shard_map/ppermute | solution.py:25
  110.3 4.3 %collective-permute-start.15 = (f32[8,2048]{1,0:T(8,128)S(1)}, f32[8,2048]{1,0:T(8,128)S(1)}, u32[]{:S(2)}, u32[]{:S(2)}) collective-permute-start(f32[8,2048]{1,0:T(8,128)S(1)} %fusion.7), channel_id=1, source_target_pairs={{0,7},{1,0},{2,1},{3,2},{4,3},{5,4},{6,5},{7,6},{8,15},{9,8},{10,9... | collective-permute-start | bytes 196616 | tf_op jit(solution)/shard_map/ppermute | solution.py:25
  114.7 7.4 %collective-permute-start.16 = (f32[8,2048]{1,0:T(8,128)S(1)}, f32[8,2048]{1,0:T(8,128)S(1)}, u32[]{:S(2)}, u32[]{:S(2)}) collective-permute-start(f32[8,2048]{1,0:T(8,128)S(1)} %get-tuple-element.36), channel_id=1, source_target_pairs={{0,3},{1,4},{2,5},{3,6},{4,7},{5,0},{6,1},{7,2},{8,11},{9,12},{10,... | collective-permute-start | bytes 196616 | tf_op jit(solution)/shard_map/ppermute | solution.py:25
  115.5 7.4 %collective-permute-start.17 = (f32[8,2048]{1,0:T(8,128)S(1)}, f32[8,2048]{1,0:T(8,128)S(1)}, u32[]{:S(2)}, u32[]{:S(2)}) collective-permute-start(f32[8,2048]{1,0:T(8,128)S(1)} %get-tuple-element.37), channel_id=1, source_target_pairs={{0,5},{1,6},{2,7},{3,0},{4,1},{5,2},{6,3},{7,4},{8,13},{9,14},{10,... | collective-permute-start | bytes 196616 | tf_op jit(solution)/shard_map/ppermute | solution.py:25
  132.7 19.0 %collective-permute-start.18 = (bf16[256,512]{1,0:T(8,128)(2,1)S(1)}, bf16[256,512]{1,0:T(8,128)(2,1)S(1)}, u32[]{:S(2)}, u32[]{:S(2)}) collective-permute-start(bf16[256,512]{1,0:T(8,128)(2,1)S(1)} %get-tuple-element.48), channel_id=1, source_target_pairs={{0,8},{8,16},{16,24},{24,0},{1,9},{9,17},{17,25},{25,1},{2,10},{10... | collective-permute-start | bytes 786440 | tf_op jit(solution)/shard_map/ppermute | solution.py:25
  133.4 18.2 %collective-permute-start.19 = (bf16[256,512]{1,0:T(8,128)(2,1)S(1)}, bf16[256,512]{1,0:T(8,128)(2,1)S(1)}, u32[]{:S(2)}, u32[]{:S(2)}) collective-permute-start(bf16[256,512]{1,0:T(8,128)(2,1)S(1)} %get-tuple-element.47), channel_id=1, source_target_pairs={{0,24},{8,0},{16,8},{24,16},{1,25},{9,1},{17,9},{25,17},{2,26},{10... | collective-permute-start | bytes 786440 | tf_op jit(solution)/shard_map/ppermute | solution.py:25
  161.3 13.4 %collective-permute-start.20 = (bf16[512,512]{1,0:T(8,128)(2,1)}, bf16[512,512]{1,0:T(8,128)(2,1)}, u32[]{:S(2)}, u32[]{:S(2)}) collective-permute-start(bf16[512,512]{1,0:T(8,128)(2,1)} %get-tuple-element.33), channel_id=1, source_target_pairs={{0,8},{8,16},{16,24},{24,0},{1,9},{9,17},{17,25},{25,1},{2,10},{10... | collective-permute-start | bytes 1572872 | tf_op jit(solution)/shard_map/ppermute | solution.py:25
  161.4 13.4 %collective-permute-start.21 = (bf16[512,512]{1,0:T(8,128)(2,1)}, bf16[512,512]{1,0:T(8,128)(2,1)}, u32[]{:S(2)}, u32[]{:S(2)}) collective-permute-start(bf16[512,512]{1,0:T(8,128)(2,1)} %get-tuple-element.34), channel_id=1, source_target_pairs={{0,24},{8,0},{16,8},{24,16},{1,25},{9,1},{17,9},{25,17},{2,26},{10... | collective-permute-start | bytes 1572872 | tf_op jit(solution)/shard_map/ppermute | solution.py:25
  172.2 13.9 %copy-start.1 = (f32[1536,512]{1,0:T(8,128)S(1)}, f32[1536,512]{1,0:T(8,128)}, u32[]{:S(2)}) copy-start(f32[1536,512]{1,0:T(8,128)} %gallery_terms.1) | copy-start | bytes 9437188
  174.8 11.4 %collective-permute-start.22 = (bf16[4,192,512]{2,1,0:T(8,128)(2,1)}, bf16[4,192,512]{2,1,0:T(8,128)(2,1)}, u32[]{:S(2)}, u32[]{:S(2)}) collective-permute-start(bf16[4,192,512]{2,1,0:T(8,128)(2,1)} %fusion), channel_id=1, source_target_pairs={{0,32},{32,0},{1,33},{33,1},{2,34},{34,2},{3,35},{35,3},{4,36},{36... | collective-permute-start | bytes 2359304 | tf_op jit(solution)/shard_map/ppermute | solution.py:298
  177.3 26.6 %all-to-all-start.1 = ((bf16[8,64,512]{2,1,0:T(8,128)(2,1)}), bf16[8,64,512]{2,1,0:T(8,128)(2,1)}, u32[]{:S(2)}, u32[]{:S(2)}) async-start(bf16[8,64,512]{2,1,0:T(8,128)(2,1)} %bitcast.35), calls=%async_computation.1 | async-start | bytes 1048576 | tf_op jit(solution)/shard_map/all_to_all | solution.py:308
  188.8 8.1 %collective-permute-start.23 = (bf16[192,512]{1,0:T(8,128)(2,1)S(1)}, bf16[192,512]{1,0:T(8,128)(2,1)S(1)}, u32[]{:S(2)}, u32[]{:S(2)}) collective-permute-start(bf16[192,512]{1,0:T(8,128)(2,1)S(1)} %get-tuple-element.42), channel_id=1, source_target_pairs={{0,64},{64,128},{128,192},{192,0},{1,65},{65,129},{129,193},{193,1... | collective-permute-start | bytes 589832 | tf_op jit(solution)/shard_map/ppermute | solution.py:25
  190.3 11.7 %collective-permute-start.24 = (bf16[192,512]{1,0:T(8,128)(2,1)S(1)}, bf16[192,512]{1,0:T(8,128)(2,1)S(1)}, u32[]{:S(2)}, u32[]{:S(2)}) collective-permute-start(bf16[192,512]{1,0:T(8,128)(2,1)S(1)} %get-tuple-element.44), channel_id=1, source_target_pairs={{0,128},{64,192},{128,0},{192,64},{1,129},{65,193},{129,1},{193,65... | collective-permute-start | bytes 589832 | tf_op jit(solution)/shard_map/ppermute | solution.py:25
  193.1 8.9 %collective-permute-start.25 = (bf16[192,512]{1,0:T(8,128)(2,1)S(1)}, bf16[192,512]{1,0:T(8,128)(2,1)S(1)}, u32[]{:S(2)}, u32[]{:S(2)}) collective-permute-start(bf16[192,512]{1,0:T(8,128)(2,1)S(1)} %get-tuple-element.43), channel_id=1, source_target_pairs={{0,192},{64,0},{128,64},{192,128},{1,193},{65,1},{129,65},{193,129... | collective-permute-start | bytes 589832 | tf_op jit(solution)/shard_map/ppermute | solution.py:25
  (7 other events, 22.2 us)
where the time goes:
time: 209 us; the launch traced here: 206 us
  Pallas kernels  70.8 us (34%)
  starting transfers between devices  61.6 us (29%)
  waiting for transfers between devices  47.3 us (23%)
  other arithmetic  13.7 us (7%)
  local copies, waits for them, and re-layouts  11.4 us (5%)
    ppermute x25, starting transfers between devices, shift(): lax.ppermute(value, axis, [(i, (i + step) % peers) for i in range(peers)])  44.6 us
    ppermute x25, waiting for transfers between devices, shift(): lax.ppermute(value, axis, [(i, (i + step) % peers) for i in range(peers)])  34.4 us
    pallas_call x3, Pallas kernels, weight_blocks(): pl.pallas_call(weight_body, grid=(steps * len(which),), in_specs=in_specs...  30 us
    pallas_call x4, Pallas kernels, score_block(): pl.pallas_call(score_body, grid=(steps,), in_specs=in_specs, out_specs=[p...  20.5 us
    all_to_all x1, waiting for transfers between devices, shard_terms(): own = lax.all_to_all(copies, 'z', 0, 0, tiled=True).reshape(size, width)  12.9 us
    pallas_call x1, Pallas kernels, rank_sums(): pl.pallas_call(rank_body, grid=(count // TILE,), in_specs=[pl.BlockSpec((...  12.6 us
    all_to_all x1, starting transfers between devices, shard_terms(): lax.all_to_all(query_part.reshape(nz, size // nz, width), 'z', 0, 0, tile...  8.82 us
    all_to_all x1, starting transfers between devices, shard_terms(): own = lax.all_to_all(copies, 'z', 0, 0, tiled=True).reshape(size, width)  8.11 us
  transfers between devices with their start and end apart: 28, of which 16 were waited for; matrix products, arithmetic and copies ran while one was open for 7% of the time, Pallas kernels for 18%

commit v1 on v0

--- a/solution.py
+++ b/solution.py
@@ -18,6 +18,10 @@
 
 def priced(micros):
     return pl.CostEstimate(flops=int(micros * 5e8), transcendentals=0, bytes_accessed=int(micros * 1e6))
+
+
+def near(value):
+    return pltpu.with_memory_space_constraint(value, pltpu.MemorySpace.VMEM)
 
 
 def shift(value, axis, step):
@@ -84,6 +88,7 @@
         ],
         input_output_aliases=aliases,
         cost_estimate=priced(5),
+        compiler_params=pltpu.CompilerParams(vmem_limit_bytes=12 * 2**20),
     )(*args)
 
 
@@ -125,6 +130,7 @@
         out_specs=pl.BlockSpec((2 * members, TILE), lambda i: (0, i)),
         out_shape=jax.ShapeDtypeStruct((2 * members, count), F32),
         cost_estimate=priced(12),
+        compiler_params=pltpu.CompilerParams(vmem_limit_bytes=8 * 2**20),
         name="rank_sums",
     )(scores, anchors)
 
@@ -202,6 +208,7 @@
         scratch_shapes=[pltpu.VMEM((2 * members, TILE), F32)],
         input_output_aliases=aliases,
         cost_estimate=priced(6 * len(which)),
+        compiler_params=pltpu.CompilerParams(vmem_limit_bytes=16 * 2**20),
     )(*args)
 
 
@@ -231,6 +238,7 @@
         out_specs=pl.BlockSpec((tile, width), lambda i: (i, 0)),
         out_shape=jax.ShapeDtypeStruct((rows, width), F32),
         cost_estimate=priced(6),
+        compiler_params=pltpu.CompilerParams(vmem_limit_bytes=20 * 2**20),
         name="gallery_terms",
     )(dscore, *parts)
 
@@ -266,21 +274,25 @@
     far_a = shift(after[:half], "y", -1)
     far_b = shift(before[half:], "y", 1)
     far = jnp.concatenate([far_a, far_b], axis=0)
-    blocks = [own, after, far, before]
+    blocks = [near(block) for block in (own, after, far, before)]
 
     scores = None
     anchors = [None] * ny
     for slot in (0, 1, 3, 2):
         index = local[:, slot * size : (slot + 1) * size]
         scores, anchors[slot] = score_block(gallery, blocks[slot], index, scores, slot, ny)
+    stored = pltpu.with_memory_space_constraint(scores, pltpu.MemorySpace.HBM)
+    scores = near(scores)
     anchors = summed_over_gallery(jnp.concatenate(anchors, axis=1))
     stats = summed_over_gallery(rank_sums(scores, anchors))
 
-    weights = functools.partial(weight_blocks, cutoffs, scores, anchors, local, stats, gallery.T)
+    weights = functools.partial(weight_blocks, cutoffs, stored, anchors, local, stats, gallery.T)
     dscore, part_far = weights(None, (2,), ny, BF16)
+    dscore = near(dscore)
     got_a = shift(part_far[:half], "y", 1)
     got_b = shift(part_far[half:], "y", -1)
     dscore, part_next = weights(dscore, (1, 3), ny, F32)
+    dscore = near(dscore)
     part_after, part_before = part_next[:size], part_next[size:]
     up = jnp.concatenate([part_after[:half] + got_a.astype(F32), part_after[half:]], axis=0).astype(BF16)
     down = jnp.concatenate([part_before[:half], part_before[half:] + got_b.astype(F32)], axis=0).astype(BF16)
@@ -288,7 +300,7 @@
     got_up = shift(up, "y", 1)
     got_down = shift(down, "y", -1)
     dscore, part_own = weights(dscore, (0,), ny, F32)
-    gallery_part = gallery_terms(dscore, blocks)
+    gallery_part = gallery_terms(near(dscore), blocks)
 
     out_rows = gallery_rows // (2 * nx)
     split = gallery_part.reshape(nx, 2, out_rows, width)

time: 209 us -> 182 us (0.87); the launches traced: 206 us -> 181 us
  Pallas kernels: 70.8 us -> 52.1 us
  other arithmetic: 13.7 us -> 7.29 us
  waiting for transfers between devices: 47.3 us -> 53.6 us
  local copies, waits for them, and re-layouts: 11.4 us -> 6.31 us
    pallas_call x4, Pallas kernels: 20.5 us -> 10.4 us  [score_block(): pl.pallas_call(score_body, grid=(steps,), in_specs=in_specs, out_specs=[p...]
    ppermute x25, waiting for transfers between devices: 34.4 us -> 40.7 us  [shift(): lax.ppermute(value, axis, [(i, (i + step) % peers) for i in range(peers)])]
    pallas_call x1, Pallas kernels: 7.6 us -> 3.76 us  [gallery_terms(): pl.pallas_call(gallery_body, grid=(rows // tile,), in_specs=[pl.BlockSpec...]
    pallas_call x3, Pallas kernels: 30 us -> 26.9 us  [weight_blocks(): pl.pallas_call(weight_body, grid=(steps * len(which),), in_specs=in_specs...]
    unnamed x27 -> x31, local copies, waits for them, and re-layouts: 5.33 us -> 3.36 us
  transfers between devices with their start and end apart: 28 -> 28, of which waited for: 16 -> 19; matrix products, arithmetic and copies ran while one was open for 7% -> 4% of each run, Pallas kernels for 18% -> 13%
where the time goes in v1:
time: 182 us; the launch traced here: 181 us
  starting transfers between devices  60.6 us (33%)
  waiting for transfers between devices  53.6 us (29%)
  Pallas kernels  52.1 us (29%)
  other arithmetic  7.29 us (4%)
  local copies, waits for them, and re-layouts  6.31 us (3%)
    ppermute x25, starting transfers between devices, shift(): lax.ppermute(value, axis, [(i, (i + step) % peers) for i in range(peers)])  44.2 us
    ppermute x25, waiting for transfers between devices, shift(): lax.ppermute(value, axis, [(i, (i + step) % peers) for i in range(peers)])  40.7 us
    pallas_call x3, Pallas kernels, weight_blocks(): pl.pallas_call(weight_body, grid=(steps * len(which),), in_specs=in_specs...  26.9 us
    all_to_all x1, waiting for transfers between devices, shard_terms(): own = lax.all_to_all(copies, 'z', 0, 0, tiled=True).reshape(size, width)  13 us
    pallas_call x1, Pallas kernels, rank_sums(): pl.pallas_call(rank_body, grid=(count // TILE,), in_specs=[pl.BlockSpec((...  10.9 us
    pallas_call x4, Pallas kernels, score_block(): pl.pallas_call(score_body, grid=(steps,), in_specs=in_specs, out_specs=[p...  10.4 us
    all_to_all x1, starting transfers between devices, shard_terms(): lax.all_to_all(query_part.reshape(nz, size // nz, width), 'z', 0, 0, tile...  8.36 us
    all_to_all x1, starting transfers between devices, shard_terms(): own = lax.all_to_all(copies, 'z', 0, 0, tiled=True).reshape(size, width)  8.11 us
  transfers between devices with their start and end apart: 28, of which 19 were waited for; matrix products, arithmetic and copies ran while one was open for 4% of the time, Pallas kernels for 13%

profile of v1, /device:TPU:64, one launch (start us, length us, event | category | flops | bytes accessed | tf_op | source)
XLA Modules:
  0.0 181.0 jit_solution(11384555810511542398)
XLA Ops:
  2.3 8.1 %all-to-all-start = ((bf16[8,64,512]{2,1,0:T(8,128)(2,1)}), bf16[8,64,512]{2,1,0:T(8,128)(2,1)S(1)}, u32[]{:S(2)}, u32[]{:S(2)}) async-start(bf16[8,64,512]{2,1,0:T(8,128)(2,1)} %broadcast_in_dim.2), calls=%async_computation | async-start | bytes 1048576 | tf_op jit(solution)/shard_map/all_to_all | solution.py:270
  11.2 13.0 %all-to-all-done = bf16[8,64,512]{2,1,0:T(8,128)(2,1)S(1)} async-done(((bf16[8,64,512]{2,1,0:T(8,128)(2,1)}), bf16[8,64,512]{2,1,0:T(8,128)(2,1)S(1)}, u32[]{:S(2)}, u32[]{:S(2)}) %all-to-all-start) | async-done | bytes 524320 | tf_op jit(solution)/shard_map/all_to_all | solution.py:270
  24.2 3.0 %collective-permute-start = (bf16[512,512]{1,0:T(8,128)(2,1)S(1)}, bf16[512,512]{1,0:T(8,128)(2,1)S(1)}, u32[]{:S(2)}, u32[]{:S(2)}) collective-permute-start(bf16[512,512]{1,0:T(8,128)(2,1)S(1)} %bitcast.31), channel_id=1, source_target_pairs={{0,24},{8,0},{16,8},{24,16},{1,25},{9,1},{17,9},{25,17},{2,26},{10... | collective-permute-start | bytes 1572872 | tf_op jit(solution)/shard_map/ppermute | solution.py:29
  28.6 2.6 %shard_map.59 = (f32[1536,2048]{1,0:T(8,128)S(1)}, f32[4,512]{1,0:T(4,128)S(1)}) custom-call(bf16[1536,512]{1,0:T(8,128)(2,1)S(1)} %copy-done.1, bf16[512,512]{1,0:T(8,128)(2,1)S(1)} %bitcast.33, s32[4,512]{1,0:T(4,128)S(1)} %get-tuple-element.56.refs_2_), custom_call_target="tpu_custom_call" | custom-call | flops 2500000000 | bytes 5000000 | tf_op jit(solution)/shard_map/pallas_call | solution.py:77
  31.3 6.1 %collective-permute-done.refs_2_.refs_1_ = bf16[512,512]{1,0:T(8,128)(2,1)S(1)} collective-permute-done((bf16[512,512]{1,0:T(8,128)(2,1)S(1)}, bf16[512,512]{1,0:T(8,128)(2,1)S(1)}, u32[]{:S(2)}, u32[]{:S(2)}) %collective-permute-start) | collective-permute-done | bytes 524320 | tf_op jit(solution)/shard_map/ppermute | solution.py:29
  37.4 3.8 %collective-permute-start.2 = (bf16[256,512]{1,0:T(8,128)(2,1)S(1)}, bf16[256,512]{1,0:T(8,128)(2,1)S(1)}, u32[]{:S(2)}, u32[]{:S(2)}) collective-permute-start(bf16[256,512]{1,0:T(8,128)(2,1)S(1)} %slice.119), channel_id=1, source_target_pairs={{0,24},{8,0},{16,8},{24,16},{1,25},{9,1},{17,9},{25,17},{2,26},{10... | collective-permute-start | bytes 786440 | tf_op jit(solution)/shard_map/ppermute | solution.py:29
  41.3 2.6 %shard_map.60 = (f32[1536,2048]{1,0:T(8,128)S(1)}, f32[4,512]{1,0:T(4,128)S(1)}) custom-call(f32[1536,2048]{1,0:T(8,128)S(1)} %get-tuple-element.19.refs_0_, bf16[1536,512]{1,0:T(8,128)(2,1)S(1)} %copy-done.1, bf16[512,512]{1,0:T(8,128)(2,1)S(1)} %collective-permute-done.refs_2_.refs_1_, ...), custom_call_target="tpu_custom_call", output_to_operand_aliasing={{0}: (0, {})} | custom-call | flops 2500000000 | bytes 5000000 | tf_op jit(solution)/shard_map/pallas_call | solution.py:77
  43.9 2.6 %shard_map.61 = (f32[1536,2048]{1,0:T(8,128)S(1)}, f32[4,512]{1,0:T(4,128)S(1)}) custom-call(f32[1536,2048]{1,0:T(8,128)S(1)} %get-tuple-element.20.refs_0_, bf16[1536,512]{1,0:T(8,128)(2,1)S(1)} %copy-done.1, bf16[512,512]{1,0:T(8,128)(2,1)S(1)} %collective-permute-done.1.refs_2_.refs_3_, ...), custom_call_target="tpu_custom_call", output_to_operand_aliasing={{0}: (0, {})} | custom-call | flops 2500000000 | bytes 5000000 | tf_op jit(solution)/shard_map/pallas_call | solution.py:77
  46.6 2.3 %collective-permute-done.3 = bf16[256,512]{1,0:T(8,128)(2,1)S(1)} collective-permute-done((bf16[256,512]{1,0:T(8,128)(2,1)S(1)}, bf16[256,512]{1,0:T(8,128)(2,1)S(1)}, u32[]{:S(2)}, u32[]{:S(2)}) %collective-permute-start.3) | collective-permute-done | bytes 262176 | tf_op jit(solution)/shard_map/ppermute | solution.py:29
  48.9 2.6 %shard_map.62 = (f32[1536,2048]{1,0:T(8,128)S(1)}, f32[4,512]{1,0:T(4,128)S(1)}) custom-call(f32[1536,2048]{1,0:T(8,128)S(1)} %get-tuple-element.21.refs_0_, bf16[1536,512]{1,0:T(8,128)(2,1)S(1)} %copy-done.1, bf16[512,512]{1,0:T(8,128)(2,1)S(1)} %constant_dynamic-update-slice_fusion.refs_2_, ...), custom_call_target="tpu_custom_call", output_to_operand_aliasing={{0}: (0, {})} | custom-call | flops 2500000000 | bytes 5000000 | tf_op jit(solution)/shard_map/pallas_call | solution.py:77
  51.7 3.2 %collective-permute-start.6 = (f32[4,2048]{1,0:T(4,128)S(1)}, f32[4,2048]{1,0:T(4,128)S(1)}, u32[]{:S(2)}, u32[]{:S(2)}) collective-permute-start(f32[4,2048]{1,0:T(4,128)S(1)} %constant_dynamic-update-slice_fusion.2), channel_id=1, source_target_pairs={{0,24},{8,0},{16,8},{24,16},{1,25},{9,1},{17,9},{25,17},{2,26},{10... | collective-permute-start | bytes 98312 | tf_op jit(solution)/shard_map/ppermute | solution.py:29
  56.8 3.5 %collective-permute-done.5 = f32[4,2048]{1,0:T(4,128)S(1)} collective-permute-done((f32[4,2048]{1,0:T(4,128)S(1)}, f32[4,2048]{1,0:T(4,128)S(1)}, u32[]{:S(2)}, u32[]{:S(2)}) %collective-permute-start.5) | collective-permute-done | bytes 32800 | tf_op jit(solution)/shard_map/ppermute | solution.py:29
  65.1 8.8 %collective-permute-start.10 = (f32[4,2048]{1,0:T(4,128)S(1)}, f32[4,2048]{1,0:T(4,128)S(1)}, u32[]{:S(2)}, u32[]{:S(2)}) collective-permute-start(f32[4,2048]{1,0:T(4,128)S(1)} %get-tuple-element.39), channel_id=1, source_target_pairs={{0,5},{1,6},{2,7},{3,0},{4,1},{5,2},{6,3},{7,4},{8,13},{9,14},{10,... | collective-permute-start | bytes 98312 | tf_op jit(solution)/shard_map/ppermute | solution.py:29
  75.5 5.3 %collective-permute-done.9 = f32[4,2048]{1,0:T(4,128)S(1)} collective-permute-done((f32[4,2048]{1,0:T(4,128)S(1)}, f32[4,2048]{1,0:T(4,128)S(1)}, u32[]{:S(2)}, u32[]{:S(2)}) %collective-permute-start.9) | collective-permute-done | bytes 32800 | tf_op jit(solution)/shard_map/ppermute | solution.py:29
  80.9 10.9 %rank_sums.1 = f32[8,2048]{1,0:T(8,128)S(1)} custom-call(f32[1536,2048]{1,0:T(8,128)S(1)} %get-tuple-element.22.score_ref.refs_1_.refs_2_, f32[4,2048]{1,0:T(4,128)S(1)} %add_add_fusion.1.anchor_ref.refs_2_.refs_3_), custom_call_target="tpu_custom_call" | custom-call | flops 6000000000 | bytes 12000000 | tf_op jit(solution)/shard_map/rank_sums/pallas_call | solution.py:123
  92.1 3.2 %collective-permute-start.13 = (f32[8,2048]{1,0:T(8,128)S(1)}, f32[8,2048]{1,0:T(8,128)S(1)}, u32[]{:S(2)}, u32[]{:S(2)}) collective-permute-start(f32[8,2048]{1,0:T(8,128)S(1)} %rank_sums.1), channel_id=1, source_target_pairs={{0,24},{8,0},{16,8},{24,16},{1,25},{9,1},{17,9},{25,17},{2,26},{10... | collective-permute-start | bytes 196616 | tf_op jit(solution)/shard_map/ppermute | solution.py:29
  95.4 2.2 %collective-permute-done.11 = f32[8,2048]{1,0:T(8,128)S(1)} collective-permute-done((f32[8,2048]{1,0:T(8,128)S(1)}, f32[8,2048]{1,0:T(8,128)S(1)}, u32[]{:S(2)}, u32[]{:S(2)}) %collective-permute-start.11) | collective-permute-done | bytes 65568 | tf_op jit(solution)/shard_map/ppermute | solution.py:29
  97.9 3.2 %collective-permute-done.12 = f32[8,2048]{1,0:T(8,128)S(1)} collective-permute-done((f32[8,2048]{1,0:T(8,128)S(1)}, f32[8,2048]{1,0:T(8,128)S(1)}, u32[]{:S(2)}, u32[]{:S(2)}) %collective-permute-start.12) | collective-permute-done | bytes 65568 | tf_op jit(solution)/shard_map/ppermute | solution.py:29
  101.3 2.0 %collective-permute-start.15 = (f32[8,2048]{1,0:T(8,128)S(1)}, f32[8,2048]{1,0:T(8,128)S(1)}, u32[]{:S(2)}, u32[]{:S(2)}) collective-permute-start(f32[8,2048]{1,0:T(8,128)S(1)} %fusion.7), channel_id=1, source_target_pairs={{0,7},{1,0},{2,1},{3,2},{4,3},{5,4},{6,5},{7,6},{8,15},{9,8},{10,9... | collective-permute-start | bytes 196616 | tf_op jit(solution)/shard_map/ppermute | solution.py:29
  103.3 2.2 %collective-permute-done.14 = f32[8,2048]{1,0:T(8,128)S(1)} collective-permute-done((f32[8,2048]{1,0:T(8,128)S(1)}, f32[8,2048]{1,0:T(8,128)S(1)}, u32[]{:S(2)}, u32[]{:S(2)}) %collective-permute-start.14) | collective-permute-done | bytes 65568 | tf_op jit(solution)/shard_map/ppermute | solution.py:29
  105.9 4.9 %collective-permute-start.17 = (f32[8,2048]{1,0:T(8,128)S(1)}, f32[8,2048]{1,0:T(8,128)S(1)}, u32[]{:S(2)}, u32[]{:S(2)}) collective-permute-start(f32[8,2048]{1,0:T(8,128)S(1)} %get-tuple-element.37), channel_id=1, source_target_pairs={{0,5},{1,6},{2,7},{3,0},{4,1},{5,2},{6,3},{7,4},{8,13},{9,14},{10,... | collective-permute-start | bytes 196616 | tf_op jit(solution)/shard_map/ppermute | solution.py:29
  113.2 7.1 %shard_map.63 = (bf16[1536,2048]{1,0:T(8,128)(2,1)S(1)}, bf16[512,512]{1,0:T(8,128)(2,1)S(1)}) custom-call(s32[4]{0:T(128)S(1)} %copy-done.11, f32[1536,2048]{1,0:T(8,128)} %copy-done, f32[4,2048]{1,0:T(4,128)S(1)} %add_add_fusion.1.anchor_ref.refs_2_.refs_3_, s32[4,2048]{1,0:T(4,128)S(1)} %fusion.8.refs_3_.refs_4_, ...), custom_call_target="tpu_custom_call" | custom-call | flops 3000000000 | bytes 6000000 | tf_op jit(solution)/shard_map/pallas_call | solution.py:199
  120.4 3.2 %collective-permute-start.19 = (bf16[256,512]{1,0:T(8,128)(2,1)S(1)}, bf16[256,512]{1,0:T(8,128)(2,1)S(1)}, u32[]{:S(2)}, u32[]{:S(2)}) collective-permute-start(bf16[256,512]{1,0:T(8,128)(2,1)S(1)} %get-tuple-element.47), channel_id=1, source_target_pairs={{0,24},{8,0},{16,8},{24,16},{1,25},{9,1},{17,9},{25,17},{2,26},{10... | collective-permute-start | bytes 786440 | tf_op jit(solution)/shard_map/ppermute | solution.py:29
  123.6 12.7 %shard_map.64 = (bf16[1536,2048]{1,0:T(8,128)(2,1)S(1)}, f32[1024,512]{1,0:T(8,128)S(1)}) custom-call(bf16[1536,2048]{1,0:T(8,128)(2,1)S(1)} %get-tuple-element.27.refs_0_, s32[4]{0:T(128)S(1)} %copy-done.11, f32[1536,2048]{1,0:T(8,128)} %copy-done, f32[4,2048]{1,0:T(4,128)S(1)} %add_add_fusion.1.anchor_ref.refs_2_.refs_3_, ...), custom_call_target="tpu_custom_call", output_to_operand_aliasing={{0}: (0, {})} | custom-call | flops 6000000000 | bytes 12000000 | tf_op jit(solution)/shard_map/pallas_call | solution.py:199
  136.8 7.2 %shard_map.65 = (bf16[1536,2048]{1,0:T(8,128)(2,1)S(1)}, f32[512,512]{1,0:T(8,128)S(1)}) custom-call(bf16[1536,2048]{1,0:T(8,128)(2,1)S(1)} %get-tuple-element.31.refs_0_, s32[4]{0:T(128)S(1)} %copy-done.11, f32[1536,2048]{1,0:T(8,128)} %copy-done, f32[4,2048]{1,0:T(4,128)S(1)} %add_add_fusion.1.anchor_ref.refs_2_.refs_3_, ...), custom_call_target="tpu_custom_call", output_to_operand_aliasing={{0}: (0, {})} | custom-call | flops 3000000000 | bytes 6000000 | tf_op jit(solution)/shard_map/pallas_call | solution.py:199
  144.1 3.2 %collective-permute-start.21 = (bf16[512,512]{1,0:T(8,128)(2,1)S(1)}, bf16[512,512]{1,0:T(8,128)(2,1)S(1)}, u32[]{:S(2)}, u32[]{:S(2)}) collective-permute-start(bf16[512,512]{1,0:T(8,128)(2,1)S(1)} %get-tuple-element.34), channel_id=1, source_target_pairs={{0,24},{8,0},{16,8},{24,16},{1,25},{9,1},{17,9},{25,17},{2,26},{10... | collective-permute-start | bytes 1572872 | tf_op jit(solution)/shard_map/ppermute | solution.py:29
  147.3 3.8 %gallery_terms.1 = f32[1536,512]{1,0:T(8,128)S(1)} custom-call(bf16[1536,2048]{1,0:T(8,128)(2,1)S(1)} %get-tuple-element.35.dscore_ref, bf16[512,512]{1,0:T(8,128)(2,1)S(1)} %bitcast.34, bf16[512,512]{1,0:T(8,128)(2,1)S(1)} %copy-done.4, bf16[512,512]{1,0:T(8,128)(2,1)S(1)} %copy-done.8, bf16[512,512]{1,0:T(8,128)(2,1)S(1)} %copy-done.6), custom_call_target="tpu_custom_call" | custom-call | flops 3000000000 | bytes 6000000 | tf_op jit(solution)/shard_map/gallery_terms/pallas_call | solution.py:231
  152.1 2.3 %collective-permute-done.20 = bf16[512,512]{1,0:T(8,128)(2,1)S(1)} collective-permute-done((bf16[512,512]{1,0:T(8,128)(2,1)S(1)}, bf16[512,512]{1,0:T(8,128)(2,1)S(1)}, u32[]{:S(2)}, u32[]{:S(2)}) %collective-permute-start.20) | collective-permute-done | bytes 524320 | tf_op jit(solution)/shard_map/ppermute | solution.py:29
  155.5 8.4 %all-to-all-start.1 = ((bf16[8,64,512]{2,1,0:T(8,128)(2,1)}), bf16[8,64,512]{2,1,0:T(8,128)(2,1)}, u32[]{:S(2)}, u32[]{:S(2)}) async-start(bf16[8,64,512]{2,1,0:T(8,128)(2,1)} %bitcast.35), calls=%async_computation.1 | async-start | bytes 1048576 | tf_op jit(solution)/shard_map/all_to_all | solution.py:320
  168.1 2.7 %collective-permute-start.24 = (bf16[192,512]{1,0:T(8,128)(2,1)S(1)}, bf16[192,512]{1,0:T(8,128)(2,1)S(1)}, u32[]{:S(2)}, u32[]{:S(2)}) collective-permute-start(bf16[192,512]{1,0:T(8,128)(2,1)S(1)} %get-tuple-element.44), channel_id=1, source_target_pairs={{0,128},{64,192},{128,0},{192,64},{1,129},{65,193},{129,1},{193,65... | collective-permute-start | bytes 589832 | tf_op jit(solution)/shard_map/ppermute | solution.py:29
  172.2 3.1 %collective-permute-done.23 = bf16[192,512]{1,0:T(8,128)(2,1)S(1)} collective-permute-done((bf16[192,512]{1,0:T(8,128)(2,1)S(1)}, bf16[192,512]{1,0:T(8,128)(2,1)S(1)}, u32[]{:S(2)}, u32[]{:S(2)}) %collective-permute-start.23) | collective-permute-done | bytes 196640 | tf_op jit(solution)/shard_map/ppermute | solution.py:29
  175.3 2.1 %collective-permute-done.24 = bf16[192,512]{1,0:T(8,128)(2,1)S(1)} collective-permute-done((bf16[192,512]{1,0:T(8,128)(2,1)S(1)}, bf16[192,512]{1,0:T(8,128)(2,1)S(1)}, u32[]{:S(2)}, u32[]{:S(2)}) %collective-permute-start.24) | collective-permute-done | bytes 196640 | tf_op jit(solution)/shard_map/ppermute | solution.py:29
  (99 shorter events, 27.8 us)
Async XLA Ops:
  2.3 21.9 %all-to-all-start = ((bf16[8,64,512]{2,1,0:T(8,128)(2,1)}), bf16[8,64,512]{2,1,0:T(8,128)(2,1)S(1)}, u32[]{:S(2)}, u32[]{:S(2)}) async-start(bf16[8,64,512]{2,1,0:T(8,128)(2,1)} %broadcast_in_dim.2), calls=%async_computation | async-start | bytes 1048576 | tf_op jit(solution)/shard_map/all_to_all | solution.py:270
  24.2 13.2 %collective-permute-start = (bf16[512,512]{1,0:T(8,128)(2,1)S(1)}, bf16[512,512]{1,0:T(8,128)(2,1)S(1)}, u32[]{:S(2)}, u32[]{:S(2)}) collective-permute-start(bf16[512,512]{1,0:T(8,128)(2,1)S(1)} %bitcast.31), channel_id=1, source_target_pairs={{0,24},{8,0},{16,8},{24,16},{1,25},{9,1},{17,9},{25,17},{2,26},{10... | collective-permute-start | bytes 1572872 | tf_op jit(solution)/shard_map/ppermute | solution.py:29
  27.2 14.0 %collective-permute-start.1 = (bf16[512,512]{1,0:T(8,128)(2,1)S(1)}, bf16[512,512]{1,0:T(8,128)(2,1)S(1)}, u32[]{:S(2)}, u32[]{:S(2)}) collective-permute-start(bf16[512,512]{1,0:T(8,128)(2,1)S(1)} %bitcast.32), channel_id=1, source_target_pairs={{0,8},{8,16},{16,24},{24,0},{1,9},{9,17},{17,25},{25,1},{2,10},{10... | collective-permute-start | bytes 1572872 | tf_op jit(solution)/shard_map/ppermute | solution.py:29
  37.4 9.2 %collective-permute-start.2 = (bf16[256,512]{1,0:T(8,128)(2,1)S(1)}, bf16[256,512]{1,0:T(8,128)(2,1)S(1)}, u32[]{:S(2)}, u32[]{:S(2)}) collective-permute-start(bf16[256,512]{1,0:T(8,128)(2,1)S(1)} %slice.119), channel_id=1, source_target_pairs={{0,24},{8,0},{16,8},{24,16},{1,25},{9,1},{17,9},{25,17},{2,26},{10... | collective-permute-start | bytes 786440 | tf_op jit(solution)/shard_map/ppermute | solution.py:29
  41.2 7.7 %collective-permute-start.3 = (bf16[256,512]{1,0:T(8,128)(2,1)S(1)}, bf16[256,512]{1,0:T(8,128)(2,1)S(1)}, u32[]{:S(2)}, u32[]{:S(2)}) collective-permute-start(bf16[256,512]{1,0:T(8,128)(2,1)S(1)} %slice.120), channel_id=1, source_target_pairs={{0,8},{8,16},{16,24},{24,0},{1,9},{9,17},{17,25},{25,1},{2,10},{10... | collective-permute-start | bytes 786440 | tf_op jit(solution)/shard_map/ppermute | solution.py:29
  51.5 40.3 %copy-start = (f32[1536,2048]{1,0:T(8,128)}, f32[1536,2048]{1,0:T(8,128)S(1)}, u32[]{:S(2)}) copy-start(f32[1536,2048]{1,0:T(8,128)S(1)} %get-tuple-element.22.score_ref.refs_1_.refs_2_) | copy-start | bytes 37748740
  51.6 5.2 %collective-permute-start.4 = (f32[4,2048]{1,0:T(4,128)S(1)}, f32[4,2048]{1,0:T(4,128)S(1)}, u32[]{:S(2)}, u32[]{:S(2)}) collective-permute-start(f32[4,2048]{1,0:T(4,128)S(1)} %constant_dynamic-update-slice_fusion.2), channel_id=1, source_target_pairs={{0,8},{8,16},{16,24},{24,0},{1,9},{9,17},{17,25},{25,1},{2,10},{10... | collective-permute-start | bytes 98312 | tf_op jit(solution)/shard_map/ppermute | solution.py:29
  51.7 5.1 %collective-permute-start.6 = (f32[4,2048]{1,0:T(4,128)S(1)}, f32[4,2048]{1,0:T(4,128)S(1)}, u32[]{:S(2)}, u32[]{:S(2)}) collective-permute-start(f32[4,2048]{1,0:T(4,128)S(1)} %constant_dynamic-update-slice_fusion.2), channel_id=1, source_target_pairs={{0,24},{8,0},{16,8},{24,16},{1,25},{9,1},{17,9},{25,17},{2,26},{10... | collective-permute-start | bytes 98312 | tf_op jit(solution)/shard_map/ppermute | solution.py:29
  54.9 5.4 %collective-permute-start.5 = (f32[4,2048]{1,0:T(4,128)S(1)}, f32[4,2048]{1,0:T(4,128)S(1)}, u32[]{:S(2)}, u32[]{:S(2)}) collective-permute-start(f32[4,2048]{1,0:T(4,128)S(1)} %constant_dynamic-update-slice_fusion.2), channel_id=1, source_target_pairs={{0,16},{8,24},{16,0},{24,8},{1,17},{9,25},{17,1},{25,9},{2,18},{10... | collective-permute-start | bytes 98312 | tf_op jit(solution)/shard_map/ppermute | solution.py:29
  60.3 4.0 %collective-permute-start.7 = (f32[4,2048]{1,0:T(4,128)S(1)}, f32[4,2048]{1,0:T(4,128)S(1)}, u32[]{:S(2)}, u32[]{:S(2)}) collective-permute-start(f32[4,2048]{1,0:T(4,128)S(1)} %fusion.10), channel_id=1, source_target_pairs={{0,1},{1,2},{2,3},{3,4},{4,5},{5,6},{6,7},{7,0},{8,9},{9,10},{10,1... | collective-permute-start | bytes 98312 | tf_op jit(solution)/shard_map/ppermute | solution.py:29
  61.2 3.9 %collective-permute-start.8 = (f32[4,2048]{1,0:T(4,128)S(1)}, f32[4,2048]{1,0:T(4,128)S(1)}, u32[]{:S(2)}, u32[]{:S(2)}) collective-permute-start(f32[4,2048]{1,0:T(4,128)S(1)} %fusion.10), channel_id=1, source_target_pairs={{0,7},{1,0},{2,1},{3,2},{4,3},{5,4},{6,5},{7,6},{8,15},{9,8},{10,9... | collective-permute-start | bytes 98312 | tf_op jit(solution)/shard_map/ppermute | solution.py:29
  65.1 10.4 %collective-permute-start.10 = (f32[4,2048]{1,0:T(4,128)S(1)}, f32[4,2048]{1,0:T(4,128)S(1)}, u32[]{:S(2)}, u32[]{:S(2)}) collective-permute-start(f32[4,2048]{1,0:T(4,128)S(1)} %get-tuple-element.39), channel_id=1, source_target_pairs={{0,5},{1,6},{2,7},{3,0},{4,1},{5,2},{6,3},{7,4},{8,13},{9,14},{10,... | collective-permute-start | bytes 98312 | tf_op jit(solution)/shard_map/ppermute | solution.py:29
  73.9 6.9 %collective-permute-start.9 = (f32[4,2048]{1,0:T(4,128)S(1)}, f32[4,2048]{1,0:T(4,128)S(1)}, u32[]{:S(2)}, u32[]{:S(2)}) collective-permute-start(f32[4,2048]{1,0:T(4,128)S(1)} %get-tuple-element.38), channel_id=1, source_target_pairs={{0,3},{1,4},{2,5},{3,6},{4,7},{5,0},{6,1},{7,2},{8,11},{9,12},{10,... | collective-permute-start | bytes 98312 | tf_op jit(solution)/shard_map/ppermute | solution.py:29
  80.9 29.8 %copy-start.2 = (bf16[1536,512]{1,0:T(8,128)(2,1)S(1)}, bf16[1536,512]{1,0:T(8,128)(2,1)}, u32[]{:S(2)}) copy-start(bf16[1536,512]{1,0:T(8,128)(2,1)} %refs_1_.7) | copy-start | bytes 4718596
  91.9 21.3 %copy-start.11 = (s32[4]{0:T(128)S(1)}, s32[4]{0:T(128)}, u32[]{:S(2)}) copy-start(s32[4]{0:T(128)} %refs_1_.9) | copy-start | bytes 52
  91.9 5.7 %collective-permute-start.11 = (f32[8,2048]{1,0:T(8,128)S(1)}, f32[8,2048]{1,0:T(8,128)S(1)}, u32[]{:S(2)}, u32[]{:S(2)}) collective-permute-start(f32[8,2048]{1,0:T(8,128)S(1)} %rank_sums.1), channel_id=1, source_target_pairs={{0,8},{8,16},{16,24},{24,0},{1,9},{9,17},{17,25},{25,1},{2,10},{10... | collective-permute-start | bytes 196616 | tf_op jit(solution)/shard_map/ppermute | solution.py:29
  92.1 5.7 %collective-permute-start.13 = (f32[8,2048]{1,0:T(8,128)S(1)}, f32[8,2048]{1,0:T(8,128)S(1)}, u32[]{:S(2)}, u32[]{:S(2)}) collective-permute-start(f32[8,2048]{1,0:T(8,128)S(1)} %rank_sums.1), channel_id=1, source_target_pairs={{0,24},{8,0},{16,8},{24,16},{1,25},{9,1},{17,9},{25,17},{2,26},{10... | collective-permute-start | bytes 196616 | tf_op jit(solution)/shard_map/ppermute | solution.py:29
  95.4 5.8 %collective-permute-start.12 = (f32[8,2048]{1,0:T(8,128)S(1)}, f32[8,2048]{1,0:T(8,128)S(1)}, u32[]{:S(2)}, u32[]{:S(2)}) collective-permute-start(f32[8,2048]{1,0:T(8,128)S(1)} %rank_sums.1), channel_id=1, source_target_pairs={{0,16},{8,24},{16,0},{24,8},{1,17},{9,25},{17,1},{25,9},{2,18},{10... | collective-permute-start | bytes 196616 | tf_op jit(solution)/shard_map/ppermute | solution.py:29
  101.2 4.3 %collective-permute-start.14 = (f32[8,2048]{1,0:T(8,128)S(1)}, f32[8,2048]{1,0:T(8,128)S(1)}, u32[]{:S(2)}, u32[]{:S(2)}) collective-permute-start(f32[8,2048]{1,0:T(8,128)S(1)} %fusion.7), channel_id=1, source_target_pairs={{0,1},{1,2},{2,3},{3,4},{4,5},{5,6},{6,7},{7,0},{8,9},{9,10},{10,1... | collective-permute-start | bytes 196616 | tf_op jit(solution)/shard_map/ppermute | solution.py:29
  101.3 4.3 %collective-permute-start.15 = (f32[8,2048]{1,0:T(8,128)S(1)}, f32[8,2048]{1,0:T(8,128)S(1)}, u32[]{:S(2)}, u32[]{:S(2)}) collective-permute-start(f32[8,2048]{1,0:T(8,128)S(1)} %fusion.7), channel_id=1, source_target_pairs={{0,7},{1,0},{2,1},{3,2},{4,3},{5,4},{6,5},{7,6},{8,15},{9,8},{10,9... | collective-permute-start | bytes 196616 | tf_op jit(solution)/shard_map/ppermute | solution.py:29
  105.6 7.4 %collective-permute-start.16 = (f32[8,2048]{1,0:T(8,128)S(1)}, f32[8,2048]{1,0:T(8,128)S(1)}, u32[]{:S(2)}, u32[]{:S(2)}) collective-permute-start(f32[8,2048]{1,0:T(8,128)S(1)} %get-tuple-element.36), channel_id=1, source_target_pairs={{0,3},{1,4},{2,5},{3,6},{4,7},{5,0},{6,1},{7,2},{8,11},{9,12},{10,... | collective-permute-start | bytes 196616 | tf_op jit(solution)/shard_map/ppermute | solution.py:29
  105.9 7.3 %collective-permute-start.17 = (f32[8,2048]{1,0:T(8,128)S(1)}, f32[8,2048]{1,0:T(8,128)S(1)}, u32[]{:S(2)}, u32[]{:S(2)}) collective-permute-start(f32[8,2048]{1,0:T(8,128)S(1)} %get-tuple-element.37), channel_id=1, source_target_pairs={{0,5},{1,6},{2,7},{3,0},{4,1},{5,2},{6,3},{7,4},{8,13},{9,14},{10,... | collective-permute-start | bytes 196616 | tf_op jit(solution)/shard_map/ppermute | solution.py:29
  120.3 16.2 %collective-permute-start.18 = (bf16[256,512]{1,0:T(8,128)(2,1)S(1)}, bf16[256,512]{1,0:T(8,128)(2,1)S(1)}, u32[]{:S(2)}, u32[]{:S(2)}) collective-permute-start(bf16[256,512]{1,0:T(8,128)(2,1)S(1)} %get-tuple-element.48), channel_id=1, source_target_pairs={{0,8},{8,16},{16,24},{24,0},{1,9},{9,17},{17,25},{25,1},{2,10},{10... | collective-permute-start | bytes 786440 | tf_op jit(solution)/shard_map/ppermute | solution.py:29
  120.4 16.1 %collective-permute-start.19 = (bf16[256,512]{1,0:T(8,128)(2,1)S(1)}, bf16[256,512]{1,0:T(8,128)(2,1)S(1)}, u32[]{:S(2)}, u32[]{:S(2)}) collective-permute-start(bf16[256,512]{1,0:T(8,128)(2,1)S(1)} %get-tuple-element.47), channel_id=1, source_target_pairs={{0,24},{8,0},{16,8},{24,16},{1,25},{9,1},{17,9},{25,17},{2,26},{10... | collective-permute-start | bytes 786440 | tf_op jit(solution)/shard_map/ppermute | solution.py:29
  136.8 10.6 %copy-start.4 = (bf16[512,512]{1,0:T(8,128)(2,1)S(1)}, bf16[512,512]{1,0:T(8,128)(2,1)}, u32[]{:S(2)}) copy-start(bf16[512,512]{1,0:T(8,128)(2,1)} %copy-done.3) | copy-start | bytes 1572868
  144.0 10.5 %collective-permute-start.20 = (bf16[512,512]{1,0:T(8,128)(2,1)S(1)}, bf16[512,512]{1,0:T(8,128)(2,1)S(1)}, u32[]{:S(2)}, u32[]{:S(2)}) collective-permute-start(bf16[512,512]{1,0:T(8,128)(2,1)S(1)} %get-tuple-element.33), channel_id=1, source_target_pairs={{0,8},{8,16},{16,24},{24,0},{1,9},{9,17},{17,25},{25,1},{2,10},{10... | collective-permute-start | bytes 1572872 | tf_op jit(solution)/shard_map/ppermute | solution.py:29
  144.1 10.4 %collective-permute-start.21 = (bf16[512,512]{1,0:T(8,128)(2,1)S(1)}, bf16[512,512]{1,0:T(8,128)(2,1)S(1)}, u32[]{:S(2)}, u32[]{:S(2)}) collective-permute-start(bf16[512,512]{1,0:T(8,128)(2,1)S(1)} %get-tuple-element.34), channel_id=1, source_target_pairs={{0,24},{8,0},{16,8},{24,16},{1,25},{9,1},{17,9},{25,17},{2,26},{10... | collective-permute-start | bytes 1572872 | tf_op jit(solution)/shard_map/ppermute | solution.py:29
  152.1 11.7 %collective-permute-start.22 = (bf16[4,192,512]{2,1,0:T(8,128)(2,1)}, bf16[4,192,512]{2,1,0:T(8,128)(2,1)}, u32[]{:S(2)}, u32[]{:S(2)}) collective-permute-start(bf16[4,192,512]{2,1,0:T(8,128)(2,1)} %fusion), channel_id=1, source_target_pairs={{0,32},{32,0},{1,33},{33,1},{2,34},{34,2},{3,35},{35,3},{4,36},{36... | collective-permute-start | bytes 2359304 | tf_op jit(solution)/shard_map/ppermute | solution.py:310
  155.5 23.7 %all-to-all-start.1 = ((bf16[8,64,512]{2,1,0:T(8,128)(2,1)}), bf16[8,64,512]{2,1,0:T(8,128)(2,1)}, u32[]{:S(2)}, u32[]{:S(2)}) async-start(bf16[8,64,512]{2,1,0:T(8,128)(2,1)} %bitcast.35), calls=%async_computation.1 | async-start | bytes 1048576 | tf_op jit(solution)/shard_map/all_to_all | solution.py:320
  166.5 8.8 %collective-permute-start.23 = (bf16[192,512]{1,0:T(8,128)(2,1)S(1)}, bf16[192,512]{1,0:T(8,128)(2,1)S(1)}, u32[]{:S(2)}, u32[]{:S(2)}) collective-permute-start(bf16[192,512]{1,0:T(8,128)(2,1)S(1)} %get-tuple-element.42), channel_id=1, source_target_pairs={{0,64},{64,128},{128,192},{192,0},{1,65},{65,129},{129,193},{193,1... | collective-permute-start | bytes 589832 | tf_op jit(solution)/shard_map/ppermute | solution.py:29
  168.1 9.3 %collective-permute-start.24 = (bf16[192,512]{1,0:T(8,128)(2,1)S(1)}, bf16[192,512]{1,0:T(8,128)(2,1)S(1)}, u32[]{:S(2)}, u32[]{:S(2)}) collective-permute-start(bf16[192,512]{1,0:T(8,128)(2,1)S(1)} %get-tuple-element.44), channel_id=1, source_target_pairs={{0,128},{64,192},{128,0},{192,64},{1,129},{65,193},{129,1},{193,65... | collective-permute-start | bytes 589832 | tf_op jit(solution)/shard_map/ppermute | solution.py:29
  170.8 6.6 %collective-permute-start.25 = (bf16[192,512]{1,0:T(8,128)(2,1)S(1)}, bf16[192,512]{1,0:T(8,128)(2,1)S(1)}, u32[]{:S(2)}, u32[]{:S(2)}) collective-permute-start(bf16[192,512]{1,0:T(8,128)(2,1)S(1)} %get-tuple-element.43), channel_id=1, source_target_pairs={{0,192},{64,0},{128,64},{192,128},{1,193},{65,1},{129,65},{193,129... | collective-permute-start | bytes 589832 | tf_op jit(solution)/shard_map/ppermute | solution.py:29
  (9 other events, 53.1 us)

commit v2 on v1

--- a/solution.py
+++ b/solution.py
@@ -57,12 +57,12 @@
         anchor_ref[m : m + 1, :] = jnp.sum(found[m], axis=0, keepdims=True)
 
 
-def score_block(gallery, queries, index, scores, slot, slots):
+def score_block(gallery, queries, index, carried, slot, slots):
     rows, width = gallery.shape
     count = queries.shape[0]
     members = index.shape[0]
     steps = count // TILE
-    first = scores is None
+    here = lambda i: (0, slot * steps + i)
     in_specs = [
         pl.BlockSpec((rows, width), lambda i: (0, 0)),
         pl.BlockSpec((TILE, width), lambda i: (i, 0)),
@@ -70,21 +70,21 @@
     ]
     args = [gallery, queries, index]
     aliases = {}
-    if not first:
-        in_specs = [pl.BlockSpec(memory_space=pl.ANY), *in_specs]
-        args = [scores, *args]
-        aliases = {0: 0}
+    if carried is not None:
+        in_specs = [pl.BlockSpec(memory_space=pl.ANY)] * 2 + in_specs
+        args = [*carried, *args]
+        aliases = {0: 0, 1: 1}
     return pl.pallas_call(
         score_body,
         grid=(steps,),
         in_specs=in_specs,
         out_specs=[
-            pl.BlockSpec((rows, TILE), lambda i: (0, slot * steps + i)),
-            pl.BlockSpec((members, TILE), lambda i: (0, i)),
+            pl.BlockSpec((rows, TILE), here),
+            pl.BlockSpec((members, TILE), here),
         ],
         out_shape=[
             jax.ShapeDtypeStruct((rows, slots * count), F32),
-            jax.ShapeDtypeStruct((members, count), F32),
+            jax.ShapeDtypeStruct((members, slots * count), F32),
         ],
         input_output_aliases=aliases,
         cost_estimate=priced(5),
@@ -170,7 +170,7 @@
             dscore_ref[pl.ds(base, CHUNK), span] = acc.astype(BF16)
             return carry
 
-        lax.fori_loop(0, rows // CHUNK, step, 0, unroll=2)
+        lax.fori_loop(0, rows // CHUNK, step, 0, unroll=4)
     turned = jnp.dot(gallery_ref[...], dscore_ref[...], preferred_element_type=F32)
     query_ref[...] = turned.T.astype(query_ref.dtype)
 
@@ -212,6 +212,26 @@
     )(*args)
 
 
+def join_body(part_ref, low_ref, high_ref, up_ref, down_ref):
+    half = low_ref.shape[0]
+    size = 2 * half
+    up_ref[0:half, :] = (part_ref[0:half, :] + low_ref[...].astype(F32)).astype(BF16)
+    up_ref[half:size, :] = part_ref[half:size, :].astype(BF16)
+    down_ref[0:half, :] = part_ref[size : size + half, :].astype(BF16)
+    down_ref[half:size, :] = (part_ref[size + half : 2 * size, :] + high_ref[...].astype(F32)).astype(BF16)
+
+
+def joined(part, low, high):
+    out = jax.ShapeDtypeStruct((part.shape[0] // 2, part.shape[1]), BF16)
+    return pl.pallas_call(
+        join_body,
+        out_shape=[out, out],
+        compiler_params=pltpu.CompilerParams(vmem_limit_bytes=8 * 2**20),
+        cost_estimate=priced(1),
+        name="joined",
+    )(part, low, high)
+
+
 def gallery_body(dscore_ref, *refs):
     out_ref = refs[-1]
     at = 0
@@ -276,14 +296,14 @@
     far = jnp.concatenate([far_a, far_b], axis=0)
     blocks = [near(block) for block in (own, after, far, before)]
 
-    scores = None
-    anchors = [None] * ny
+    carried = None
     for slot in (0, 1, 3, 2):
         index = local[:, slot * size : (slot + 1) * size]
-        scores, anchors[slot] = score_block(gallery, blocks[slot], index, scores, slot, ny)
+        carried = score_block(gallery, blocks[slot], index, carried, slot, ny)
+    scores, anchors = carried
     stored = pltpu.with_memory_space_constraint(scores, pltpu.MemorySpace.HBM)
     scores = near(scores)
-    anchors = summed_over_gallery(jnp.concatenate(anchors, axis=1))
+    anchors = summed_over_gallery(anchors)
     stats = summed_over_gallery(rank_sums(scores, anchors))
 
     weights = functools.partial(weight_blocks, cutoffs, stored, anchors, local, stats, gallery.T)
@@ -293,9 +313,7 @@
     got_b = shift(part_far[half:], "y", -1)
     dscore, part_next = weights(dscore, (1, 3), ny, F32)
     dscore = near(dscore)
-    part_after, part_before = part_next[:size], part_next[size:]
-    up = jnp.concatenate([part_after[:half] + got_a.astype(F32), part_after[half:]], axis=0).astype(BF16)
-    down = jnp.concatenate([part_before[:half], part_before[half:] + got_b.astype(F32)], axis=0).astype(BF16)
+    up, down = joined(part_next, got_a, got_b)
     dscore, up, down = lax.optimization_barrier((dscore, up, down))
     got_up = shift(up, "y", 1)
     got_down = shift(down, "y", -1)

time: 182 us -> 181 us (level)
  transfers between devices with their start and end apart: 28 -> 28, of which waited for: 19 -> 19; matrix products, arithmetic and copies ran while one was open for 4% -> 4% of each run, Pallas kernels for 13% -> 14%
where the time goes in v2:
time: 181 us; the launch traced here: 179 us
  starting transfers between devices  59.9 us (33%)
  waiting for transfers between devices  53.2 us (29%)
  Pallas kernels  52.2 us (29%)
  other arithmetic  6.91 us (4%)
  local copies, waits for them, and re-layouts  6.22 us (3%)
    ppermute x25, starting transfers between devices, shift(): lax.ppermute(value, axis, [(i, (i + step) % peers) for i in range(peers)])  43.5 us
    ppermute x25, waiting for transfers between devices, shift(): lax.ppermute(value, axis, [(i, (i + step) % peers) for i in range(peers)])  40.1 us
    pallas_call x3, Pallas kernels, weight_blocks(): pl.pallas_call(weight_body, grid=(steps * len(which),), in_specs=in_specs...  26.9 us
    all_to_all x1, waiting for transfers between devices, shard_terms(): own = lax.all_to_all(copies, 'z', 0, 0, tiled=True).reshape(size, width)  13 us
    pallas_call x1, Pallas kernels, rank_sums(): pl.pallas_call(rank_body, grid=(count // TILE,), in_specs=[pl.BlockSpec((...  10.9 us
    pallas_call x4, Pallas kernels, score_block(): pl.pallas_call(score_body, grid=(steps,), in_specs=in_specs, out_specs=[p...  10.4 us
    all_to_all x1, starting transfers between devices, shard_terms(): lax.all_to_all(query_part.reshape(nz, size // nz, width), 'z', 0, 0, tile...  8.35 us
    all_to_all x1, starting transfers between devices, shard_terms(): own = lax.all_to_all(copies, 'z', 0, 0, tiled=True).reshape(size, width)  8.11 us
  transfers between devices with their start and end apart: 28, of which 19 were waited for; matrix products, arithmetic and copies ran while one was open for 4% of the time, Pallas kernels for 14%

profile of v2, /device:TPU:64, one launch (start us, length us, event | category | flops | bytes accessed | tf_op | source)
XLA Modules:
  0.0 179.5 jit_solution(13970838861278539433)
XLA Ops:
  2.3 8.1 %all-to-all-start = ((bf16[8,64,512]{2,1,0:T(8,128)(2,1)}), bf16[8,64,512]{2,1,0:T(8,128)(2,1)S(1)}, u32[]{:S(2)}, u32[]{:S(2)}) async-start(bf16[8,64,512]{2,1,0:T(8,128)(2,1)} %broadcast_in_dim.2), calls=%async_computation | async-start | bytes 1048576 | tf_op jit(solution)/shard_map/all_to_all | solution.py:290
  11.2 13.0 %all-to-all-done = bf16[8,64,512]{2,1,0:T(8,128)(2,1)S(1)} async-done(((bf16[8,64,512]{2,1,0:T(8,128)(2,1)}), bf16[8,64,512]{2,1,0:T(8,128)(2,1)S(1)}, u32[]{:S(2)}, u32[]{:S(2)}) %all-to-all-start) | async-done | bytes 524320 | tf_op jit(solution)/shard_map/all_to_all | solution.py:290
  24.2 3.0 %collective-permute-start = (bf16[512,512]{1,0:T(8,128)(2,1)S(1)}, bf16[512,512]{1,0:T(8,128)(2,1)S(1)}, u32[]{:S(2)}, u32[]{:S(2)}) collective-permute-start(bf16[512,512]{1,0:T(8,128)(2,1)S(1)} %bitcast.31), channel_id=1, source_target_pairs={{0,24},{8,0},{16,8},{24,16},{1,25},{9,1},{17,9},{25,17},{2,26},{10... | collective-permute-start | bytes 1572872 | tf_op jit(solution)/shard_map/ppermute | solution.py:29
  28.7 2.6 %shard_map.59 = (f32[1536,2048]{1,0:T(8,128)S(1)}, f32[4,2048]{1,0:T(4,128)S(1)}) custom-call(bf16[1536,512]{1,0:T(8,128)(2,1)S(1)} %copy-done.1, bf16[512,512]{1,0:T(8,128)(2,1)S(1)} %bitcast.33, s32[4,512]{1,0:T(4,128)S(1)} %get-tuple-element.56.refs_2_), custom_call_target="tpu_custom_call" | custom-call | flops 2500000000 | bytes 5000000 | tf_op jit(solution)/shard_map/pallas_call | solution.py:77
  31.3 6.1 %collective-permute-done.refs_3_.refs_1_ = bf16[512,512]{1,0:T(8,128)(2,1)S(1)} collective-permute-done((bf16[512,512]{1,0:T(8,128)(2,1)S(1)}, bf16[512,512]{1,0:T(8,128)(2,1)S(1)}, u32[]{:S(2)}, u32[]{:S(2)}) %collective-permute-start) | collective-permute-done | bytes 524320 | tf_op jit(solution)/shard_map/ppermute | solution.py:29
  37.4 3.8 %collective-permute-start.2 = (bf16[256,512]{1,0:T(8,128)(2,1)S(1)}, bf16[256,512]{1,0:T(8,128)(2,1)S(1)}, u32[]{:S(2)}, u32[]{:S(2)}) collective-permute-start(bf16[256,512]{1,0:T(8,128)(2,1)S(1)} %slice.95), channel_id=1, source_target_pairs={{0,24},{8,0},{16,8},{24,16},{1,25},{9,1},{17,9},{25,17},{2,26},{10... | collective-permute-start | bytes 786440 | tf_op jit(solution)/shard_map/ppermute | solution.py:29
  41.3 2.6 %shard_map.60 = (f32[1536,2048]{1,0:T(8,128)S(1)}, f32[4,2048]{1,0:T(4,128)S(1)}) custom-call(f32[1536,2048]{1,0:T(8,128)S(1)} %get-tuple-element.21.refs_0_, f32[4,2048]{1,0:T(4,128)S(1)} %get-tuple-element.22.refs_1_, bf16[1536,512]{1,0:T(8,128)(2,1)S(1)} %copy-done.1, ...), custom_call_target="tpu_custom_call", output_to_operand_aliasing={{0}: (0, {}), {1}: (1, {})} | custom-call | flops 2500000000 | bytes 5000000 | tf_op jit(solution)/shard_map/pallas_call | solution.py:77
  43.9 2.6 %shard_map.61 = (f32[1536,2048]{1,0:T(8,128)S(1)}, f32[4,2048]{1,0:T(4,128)S(1)}) custom-call(f32[1536,2048]{1,0:T(8,128)S(1)} %get-tuple-element.23.refs_0_, f32[4,2048]{1,0:T(4,128)S(1)} %get-tuple-element.24.refs_1_, bf16[1536,512]{1,0:T(8,128)(2,1)S(1)} %copy-done.1, ...), custom_call_target="tpu_custom_call", output_to_operand_aliasing={{0}: (0, {}), {1}: (1, {})} | custom-call | flops 2500000000 | bytes 5000000 | tf_op jit(solution)/shard_map/pallas_call | solution.py:77
  46.6 2.3 %collective-permute-done.3 = bf16[256,512]{1,0:T(8,128)(2,1)S(1)} collective-permute-done((bf16[256,512]{1,0:T(8,128)(2,1)S(1)}, bf16[256,512]{1,0:T(8,128)(2,1)S(1)}, u32[]{:S(2)}, u32[]{:S(2)}) %collective-permute-start.3) | collective-permute-done | bytes 262176 | tf_op jit(solution)/shard_map/ppermute | solution.py:29
  48.9 2.6 %shard_map.62 = (f32[1536,2048]{1,0:T(8,128)S(1)}, f32[4,2048]{1,0:T(4,128)S(1)}) custom-call(f32[1536,2048]{1,0:T(8,128)S(1)} %get-tuple-element.25.refs_0_, f32[4,2048]{1,0:T(4,128)S(1)} %get-tuple-element.26.refs_1_, bf16[1536,512]{1,0:T(8,128)(2,1)S(1)} %copy-done.1, ...), custom_call_target="tpu_custom_call", output_to_operand_aliasing={{0}: (0, {}), {1}: (1, {})} | custom-call | flops 2500000000 | bytes 5000000 | tf_op jit(solution)/shard_map/pallas_call | solution.py:77
  55.5 2.1 %collective-permute-done.4 = f32[4,2048]{1,0:T(4,128)S(1)} collective-permute-done((f32[4,2048]{1,0:T(4,128)S(1)}, f32[4,2048]{1,0:T(4,128)S(1)}, u32[]{:S(2)}, u32[]{:S(2)}) %collective-permute-start.4) | collective-permute-done | bytes 32800 | tf_op jit(solution)/shard_map/ppermute | solution.py:29
  61.2 1.9 %collective-permute-done.7 = f32[4,2048]{1,0:T(4,128)S(1)} collective-permute-done((f32[4,2048]{1,0:T(4,128)S(1)}, f32[4,2048]{1,0:T(4,128)S(1)}, u32[]{:S(2)}, u32[]{:S(2)}) %collective-permute-start.7) | collective-permute-done | bytes 32800 | tf_op jit(solution)/shard_map/ppermute | solution.py:29
  63.9 8.8 %collective-permute-start.10 = (f32[4,2048]{1,0:T(4,128)S(1)}, f32[4,2048]{1,0:T(4,128)S(1)}, u32[]{:S(2)}, u32[]{:S(2)}) collective-permute-start(f32[4,2048]{1,0:T(4,128)S(1)} %get-tuple-element.43), channel_id=1, source_target_pairs={{0,5},{1,6},{2,7},{3,0},{4,1},{5,2},{6,3},{7,4},{8,13},{9,14},{10,... | collective-permute-start | bytes 98312 | tf_op jit(solution)/shard_map/ppermute | solution.py:29
  74.3 5.3 %collective-permute-done.9 = f32[4,2048]{1,0:T(4,128)S(1)} collective-permute-done((f32[4,2048]{1,0:T(4,128)S(1)}, f32[4,2048]{1,0:T(4,128)S(1)}, u32[]{:S(2)}, u32[]{:S(2)}) %collective-permute-start.9) | collective-permute-done | bytes 32800 | tf_op jit(solution)/shard_map/ppermute | solution.py:29
  79.7 10.9 %rank_sums.1 = f32[8,2048]{1,0:T(8,128)S(1)} custom-call(f32[1536,2048]{1,0:T(8,128)S(1)} %get-tuple-element.27.score_ref.refs_1_.refs_2_, f32[4,2048]{1,0:T(4,128)S(1)} %add_add_fusion.1.anchor_ref.refs_2_.refs_3_), custom_call_target="tpu_custom_call" | custom-call | flops 6000000000 | bytes 12000000 | tf_op jit(solution)/shard_map/rank_sums/pallas_call | solution.py:123
  90.9 3.2 %collective-permute-start.13 = (f32[8,2048]{1,0:T(8,128)S(1)}, f32[8,2048]{1,0:T(8,128)S(1)}, u32[]{:S(2)}, u32[]{:S(2)}) collective-permute-start(f32[8,2048]{1,0:T(8,128)S(1)} %rank_sums.1), channel_id=1, source_target_pairs={{0,24},{8,0},{16,8},{24,16},{1,25},{9,1},{17,9},{25,17},{2,26},{10... | collective-permute-start | bytes 196616 | tf_op jit(solution)/shard_map/ppermute | solution.py:29
  94.1 2.2 %collective-permute-done.11 = f32[8,2048]{1,0:T(8,128)S(1)} collective-permute-done((f32[8,2048]{1,0:T(8,128)S(1)}, f32[8,2048]{1,0:T(8,128)S(1)}, u32[]{:S(2)}, u32[]{:S(2)}) %collective-permute-start.11) | collective-permute-done | bytes 65568 | tf_op jit(solution)/shard_map/ppermute | solution.py:29
  96.4 3.5 %collective-permute-done.12 = f32[8,2048]{1,0:T(8,128)S(1)} collective-permute-done((f32[8,2048]{1,0:T(8,128)S(1)}, f32[8,2048]{1,0:T(8,128)S(1)}, u32[]{:S(2)}, u32[]{:S(2)}) %collective-permute-start.12) | collective-permute-done | bytes 65568 | tf_op jit(solution)/shard_map/ppermute | solution.py:29
  100.0 2.0 %collective-permute-start.15 = (f32[8,2048]{1,0:T(8,128)S(1)}, f32[8,2048]{1,0:T(8,128)S(1)}, u32[]{:S(2)}, u32[]{:S(2)}) collective-permute-start(f32[8,2048]{1,0:T(8,128)S(1)} %fusion.7), channel_id=1, source_target_pairs={{0,7},{1,0},{2,1},{3,2},{4,3},{5,4},{6,5},{7,6},{8,15},{9,8},{10,9... | collective-permute-start | bytes 196616 | tf_op jit(solution)/shard_map/ppermute | solution.py:29
  102.0 2.2 %collective-permute-done.14 = f32[8,2048]{1,0:T(8,128)S(1)} collective-permute-done((f32[8,2048]{1,0:T(8,128)S(1)}, f32[8,2048]{1,0:T(8,128)S(1)}, u32[]{:S(2)}, u32[]{:S(2)}) %collective-permute-start.14) | collective-permute-done | bytes 65568 | tf_op jit(solution)/shard_map/ppermute | solution.py:29
  104.6 4.9 %collective-permute-start.17 = (f32[8,2048]{1,0:T(8,128)S(1)}, f32[8,2048]{1,0:T(8,128)S(1)}, u32[]{:S(2)}, u32[]{:S(2)}) collective-permute-start(f32[8,2048]{1,0:T(8,128)S(1)} %get-tuple-element.41), channel_id=1, source_target_pairs={{0,5},{1,6},{2,7},{3,0},{4,1},{5,2},{6,3},{7,4},{8,13},{9,14},{10,... | collective-permute-start | bytes 196616 | tf_op jit(solution)/shard_map/ppermute | solution.py:29
  111.9 7.1 %shard_map.63 = (bf16[1536,2048]{1,0:T(8,128)(2,1)S(1)}, bf16[512,512]{1,0:T(8,128)(2,1)S(1)}) custom-call(s32[4]{0:T(128)S(1)} %copy-done.11, f32[1536,2048]{1,0:T(8,128)} %copy-done, f32[4,2048]{1,0:T(4,128)S(1)} %add_add_fusion.1.anchor_ref.refs_2_.refs_3_, s32[4,2048]{1,0:T(4,128)S(1)} %fusion.8.refs_3_.refs_4_, ...), custom_call_target="tpu_custom_call" | custom-call | flops 3000000000 | bytes 6000000 | tf_op jit(solution)/shard_map/pallas_call | solution.py:199
  119.1 3.2 %collective-permute-start.19 = (bf16[256,512]{1,0:T(8,128)(2,1)S(1)}, bf16[256,512]{1,0:T(8,128)(2,1)S(1)}, u32[]{:S(2)}, u32[]{:S(2)}) collective-permute-start(bf16[256,512]{1,0:T(8,128)(2,1)S(1)} %get-tuple-element.47), channel_id=1, source_target_pairs={{0,24},{8,0},{16,8},{24,16},{1,25},{9,1},{17,9},{25,17},{2,26},{10... | collective-permute-start | bytes 786440 | tf_op jit(solution)/shard_map/ppermute | solution.py:29
  122.4 12.7 %shard_map.64 = (bf16[1536,2048]{1,0:T(8,128)(2,1)S(1)}, f32[1024,512]{1,0:T(8,128)S(1)}) custom-call(bf16[1536,2048]{1,0:T(8,128)(2,1)S(1)} %get-tuple-element.29.refs_0_, s32[4]{0:T(128)S(1)} %copy-done.11, f32[1536,2048]{1,0:T(8,128)} %copy-done, f32[4,2048]{1,0:T(4,128)S(1)} %add_add_fusion.1.anchor_ref.refs_2_.refs_3_, ...), custom_call_target="tpu_custom_call", output_to_operand_aliasing={{0}: (0, {})} | custom-call | flops 6000000000 | bytes 12000000 | tf_op jit(solution)/shard_map/pallas_call | solution.py:199
  135.3 7.2 %shard_map.65 = (bf16[1536,2048]{1,0:T(8,128)(2,1)S(1)}, f32[512,512]{1,0:T(8,128)S(1)}) custom-call(bf16[1536,2048]{1,0:T(8,128)(2,1)S(1)} %get-tuple-element.35.refs_0_, s32[4]{0:T(128)S(1)} %copy-done.11, f32[1536,2048]{1,0:T(8,128)} %copy-done, f32[4,2048]{1,0:T(4,128)S(1)} %add_add_fusion.1.anchor_ref.refs_2_.refs_3_, ...), custom_call_target="tpu_custom_call", output_to_operand_aliasing={{0}: (0, {})} | custom-call | flops 3000000000 | bytes 6000000 | tf_op jit(solution)/shard_map/pallas_call | solution.py:199
  142.6 3.2 %collective-permute-start.21 = (bf16[512,512]{1,0:T(8,128)(2,1)S(1)}, bf16[512,512]{1,0:T(8,128)(2,1)S(1)}, u32[]{:S(2)}, u32[]{:S(2)}) collective-permute-start(bf16[512,512]{1,0:T(8,128)(2,1)S(1)} %get-tuple-element.38), channel_id=1, source_target_pairs={{0,24},{8,0},{16,8},{24,16},{1,25},{9,1},{17,9},{25,17},{2,26},{10... | collective-permute-start | bytes 1572872 | tf_op jit(solution)/shard_map/ppermute | solution.py:29
  145.8 3.8 %gallery_terms.1 = f32[1536,512]{1,0:T(8,128)S(1)} custom-call(bf16[1536,2048]{1,0:T(8,128)(2,1)S(1)} %get-tuple-element.39.dscore_ref, bf16[512,512]{1,0:T(8,128)(2,1)S(1)} %bitcast.34, bf16[512,512]{1,0:T(8,128)(2,1)S(1)} %copy-done.4, bf16[512,512]{1,0:T(8,128)(2,1)S(1)} %copy-done.8, bf16[512,512]{1,0:T(8,128)(2,1)S(1)} %copy-done.6), custom_call_target="tpu_custom_call" | custom-call | flops 3000000000 | bytes 6000000 | tf_op jit(solution)/shard_map/gallery_terms/pallas_call | solution.py:251
  150.6 2.4 %collective-permute-done.20 = bf16[512,512]{1,0:T(8,128)(2,1)S(1)} collective-permute-done((bf16[512,512]{1,0:T(8,128)(2,1)S(1)}, bf16[512,512]{1,0:T(8,128)(2,1)S(1)}, u32[]{:S(2)}, u32[]{:S(2)}) %collective-permute-start.20) | collective-permute-done | bytes 524320 | tf_op jit(solution)/shard_map/ppermute | solution.py:29
  153.9 8.3 %all-to-all-start.1 = ((bf16[8,64,512]{2,1,0:T(8,128)(2,1)}), bf16[8,64,512]{2,1,0:T(8,128)(2,1)}, u32[]{:S(2)}, u32[]{:S(2)}) async-start(bf16[8,64,512]{2,1,0:T(8,128)(2,1)} %bitcast.35), calls=%async_computation.1 | async-start | bytes 1048576 | tf_op jit(solution)/shard_map/all_to_all | solution.py:338
  166.5 2.7 %collective-permute-start.24 = (bf16[192,512]{1,0:T(8,128)(2,1)S(1)}, bf16[192,512]{1,0:T(8,128)(2,1)S(1)}, u32[]{:S(2)}, u32[]{:S(2)}) collective-permute-start(bf16[192,512]{1,0:T(8,128)(2,1)S(1)} %get-tuple-element.46), channel_id=1, source_target_pairs={{0,128},{64,192},{128,0},{192,64},{1,129},{65,193},{129,1},{193,65... | collective-permute-start | bytes 589832 | tf_op jit(solution)/shard_map/ppermute | solution.py:29
  170.7 3.0 %collective-permute-done.23 = bf16[192,512]{1,0:T(8,128)(2,1)S(1)} collective-permute-done((bf16[192,512]{1,0:T(8,128)(2,1)S(1)}, bf16[192,512]{1,0:T(8,128)(2,1)S(1)}, u32[]{:S(2)}, u32[]{:S(2)}) %collective-permute-start.23) | collective-permute-done | bytes 196640 | tf_op jit(solution)/shard_map/ppermute | solution.py:29
  173.7 2.1 %collective-permute-done.24 = bf16[192,512]{1,0:T(8,128)(2,1)S(1)} collective-permute-done((bf16[192,512]{1,0:T(8,128)(2,1)S(1)}, bf16[192,512]{1,0:T(8,128)(2,1)S(1)}, u32[]{:S(2)}, u32[]{:S(2)}) %collective-permute-start.24) | collective-permute-done | bytes 196640 | tf_op jit(solution)/shard_map/ppermute | solution.py:29
  (92 shorter events, 28.8 us)
Async XLA Ops:
  2.3 21.9 %all-to-all-start = ((bf16[8,64,512]{2,1,0:T(8,128)(2,1)}), bf16[8,64,512]{2,1,0:T(8,128)(2,1)S(1)}, u32[]{:S(2)}, u32[]{:S(2)}) async-start(bf16[8,64,512]{2,1,0:T(8,128)(2,1)} %broadcast_in_dim.2), calls=%async_computation | async-start | bytes 1048576 | tf_op jit(solution)/shard_map/all_to_all | solution.py:290
  24.2 13.2 %collective-permute-start = (bf16[512,512]{1,0:T(8,128)(2,1)S(1)}, bf16[512,512]{1,0:T(8,128)(2,1)S(1)}, u32[]{:S(2)}, u32[]{:S(2)}) collective-permute-start(bf16[512,512]{1,0:T(8,128)(2,1)S(1)} %bitcast.31), channel_id=1, source_target_pairs={{0,24},{8,0},{16,8},{24,16},{1,25},{9,1},{17,9},{25,17},{2,26},{10... | collective-permute-start | bytes 1572872 | tf_op jit(solution)/shard_map/ppermute | solution.py:29
  27.2 14.0 %collective-permute-start.1 = (bf16[512,512]{1,0:T(8,128)(2,1)S(1)}, bf16[512,512]{1,0:T(8,128)(2,1)S(1)}, u32[]{:S(2)}, u32[]{:S(2)}) collective-permute-start(bf16[512,512]{1,0:T(8,128)(2,1)S(1)} %bitcast.32), channel_id=1, source_target_pairs={{0,8},{8,16},{16,24},{24,0},{1,9},{9,17},{17,25},{25,1},{2,10},{10... | collective-permute-start | bytes 1572872 | tf_op jit(solution)/shard_map/ppermute | solution.py:29
  37.4 9.2 %collective-permute-start.2 = (bf16[256,512]{1,0:T(8,128)(2,1)S(1)}, bf16[256,512]{1,0:T(8,128)(2,1)S(1)}, u32[]{:S(2)}, u32[]{:S(2)}) collective-permute-start(bf16[256,512]{1,0:T(8,128)(2,1)S(1)} %slice.95), channel_id=1, source_target_pairs={{0,24},{8,0},{16,8},{24,16},{1,25},{9,1},{17,9},{25,17},{2,26},{10... | collective-permute-start | bytes 786440 | tf_op jit(solution)/shard_map/ppermute | solution.py:29
  41.2 7.7 %collective-permute-start.3 = (bf16[256,512]{1,0:T(8,128)(2,1)S(1)}, bf16[256,512]{1,0:T(8,128)(2,1)S(1)}, u32[]{:S(2)}, u32[]{:S(2)}) collective-permute-start(bf16[256,512]{1,0:T(8,128)(2,1)S(1)} %slice.96), channel_id=1, source_target_pairs={{0,8},{8,16},{16,24},{24,0},{1,9},{9,17},{17,25},{25,1},{2,10},{10... | collective-permute-start | bytes 786440 | tf_op jit(solution)/shard_map/ppermute | solution.py:29
  51.5 39.1 %copy-start = (f32[1536,2048]{1,0:T(8,128)}, f32[1536,2048]{1,0:T(8,128)S(1)}, u32[]{:S(2)}) copy-start(f32[1536,2048]{1,0:T(8,128)S(1)} %get-tuple-element.27.score_ref.refs_1_.refs_2_) | copy-start | bytes 37748740
  51.5 4.0 %collective-permute-start.6 = (f32[4,2048]{1,0:T(4,128)S(1)}, f32[4,2048]{1,0:T(4,128)S(1)}, u32[]{:S(2)}, u32[]{:S(2)}) collective-permute-start(f32[4,2048]{1,0:T(4,128)S(1)} %get-tuple-element.28), channel_id=1, source_target_pairs={{0,24},{8,0},{16,8},{24,16},{1,25},{9,1},{17,9},{25,17},{2,26},{10... | collective-permute-start | bytes 98312 | tf_op jit(solution)/shard_map/ppermute | solution.py:29
  52.6 5.1 %collective-permute-start.4 = (f32[4,2048]{1,0:T(4,128)S(1)}, f32[4,2048]{1,0:T(4,128)S(1)}, u32[]{:S(2)}, u32[]{:S(2)}) collective-permute-start(f32[4,2048]{1,0:T(4,128)S(1)} %get-tuple-element.28), channel_id=1, source_target_pairs={{0,8},{8,16},{16,24},{24,0},{1,9},{9,17},{17,25},{25,1},{2,10},{10... | collective-permute-start | bytes 98312 | tf_op jit(solution)/shard_map/ppermute | solution.py:29
  53.6 5.4 %collective-permute-start.5 = (f32[4,2048]{1,0:T(4,128)S(1)}, f32[4,2048]{1,0:T(4,128)S(1)}, u32[]{:S(2)}, u32[]{:S(2)}) collective-permute-start(f32[4,2048]{1,0:T(4,128)S(1)} %get-tuple-element.28), channel_id=1, source_target_pairs={{0,16},{8,24},{16,0},{24,8},{1,17},{9,25},{17,1},{25,9},{2,18},{10... | collective-permute-start | bytes 98312 | tf_op jit(solution)/shard_map/ppermute | solution.py:29
  59.1 4.0 %collective-permute-start.7 = (f32[4,2048]{1,0:T(4,128)S(1)}, f32[4,2048]{1,0:T(4,128)S(1)}, u32[]{:S(2)}, u32[]{:S(2)}) collective-permute-start(f32[4,2048]{1,0:T(4,128)S(1)} %fusion.10), channel_id=1, source_target_pairs={{0,1},{1,2},{2,3},{3,4},{4,5},{5,6},{6,7},{7,0},{8,9},{9,10},{10,1... | collective-permute-start | bytes 98312 | tf_op jit(solution)/shard_map/ppermute | solution.py:29
  59.9 3.9 %collective-permute-start.8 = (f32[4,2048]{1,0:T(4,128)S(1)}, f32[4,2048]{1,0:T(4,128)S(1)}, u32[]{:S(2)}, u32[]{:S(2)}) collective-permute-start(f32[4,2048]{1,0:T(4,128)S(1)} %fusion.10), channel_id=1, source_target_pairs={{0,7},{1,0},{2,1},{3,2},{4,3},{5,4},{6,5},{7,6},{8,15},{9,8},{10,9... | collective-permute-start | bytes 98312 | tf_op jit(solution)/shard_map/ppermute | solution.py:29
  63.9 10.4 %collective-permute-start.10 = (f32[4,2048]{1,0:T(4,128)S(1)}, f32[4,2048]{1,0:T(4,128)S(1)}, u32[]{:S(2)}, u32[]{:S(2)}) collective-permute-start(f32[4,2048]{1,0:T(4,128)S(1)} %get-tuple-element.43), channel_id=1, source_target_pairs={{0,5},{1,6},{2,7},{3,0},{4,1},{5,2},{6,3},{7,4},{8,13},{9,14},{10,... | collective-permute-start | bytes 98312 | tf_op jit(solution)/shard_map/ppermute | solution.py:29
  72.7 6.9 %collective-permute-start.9 = (f32[4,2048]{1,0:T(4,128)S(1)}, f32[4,2048]{1,0:T(4,128)S(1)}, u32[]{:S(2)}, u32[]{:S(2)}) collective-permute-start(f32[4,2048]{1,0:T(4,128)S(1)} %get-tuple-element.42), channel_id=1, source_target_pairs={{0,3},{1,4},{2,5},{3,6},{4,7},{5,0},{6,1},{7,2},{8,11},{9,12},{10,... | collective-permute-start | bytes 98312 | tf_op jit(solution)/shard_map/ppermute | solution.py:29
  79.6 29.8 %copy-start.2 = (bf16[1536,512]{1,0:T(8,128)(2,1)S(1)}, bf16[1536,512]{1,0:T(8,128)(2,1)}, u32[]{:S(2)}) copy-start(bf16[1536,512]{1,0:T(8,128)(2,1)} %refs_2_.5) | copy-start | bytes 4718596
  90.6 21.3 %copy-start.11 = (s32[4]{0:T(128)S(1)}, s32[4]{0:T(128)}, u32[]{:S(2)}) copy-start(s32[4]{0:T(128)} %refs_1_.3) | copy-start | bytes 52
  90.6 5.7 %collective-permute-start.11 = (f32[8,2048]{1,0:T(8,128)S(1)}, f32[8,2048]{1,0:T(8,128)S(1)}, u32[]{:S(2)}, u32[]{:S(2)}) collective-permute-start(f32[8,2048]{1,0:T(8,128)S(1)} %rank_sums.1), channel_id=1, source_target_pairs={{0,8},{8,16},{16,24},{24,0},{1,9},{9,17},{17,25},{25,1},{2,10},{10... | collective-permute-start | bytes 196616 | tf_op jit(solution)/shard_map/ppermute | solution.py:29
  90.9 5.5 %collective-permute-start.13 = (f32[8,2048]{1,0:T(8,128)S(1)}, f32[8,2048]{1,0:T(8,128)S(1)}, u32[]{:S(2)}, u32[]{:S(2)}) collective-permute-start(f32[8,2048]{1,0:T(8,128)S(1)} %rank_sums.1), channel_id=1, source_target_pairs={{0,24},{8,0},{16,8},{24,16},{1,25},{9,1},{17,9},{25,17},{2,26},{10... | collective-permute-start | bytes 196616 | tf_op jit(solution)/shard_map/ppermute | solution.py:29
  94.1 5.8 %collective-permute-start.12 = (f32[8,2048]{1,0:T(8,128)S(1)}, f32[8,2048]{1,0:T(8,128)S(1)}, u32[]{:S(2)}, u32[]{:S(2)}) collective-permute-start(f32[8,2048]{1,0:T(8,128)S(1)} %rank_sums.1), channel_id=1, source_target_pairs={{0,16},{8,24},{16,0},{24,8},{1,17},{9,25},{17,1},{25,9},{2,18},{10... | collective-permute-start | bytes 196616 | tf_op jit(solution)/shard_map/ppermute | solution.py:29
  99.9 4.3 %collective-permute-start.14 = (f32[8,2048]{1,0:T(8,128)S(1)}, f32[8,2048]{1,0:T(8,128)S(1)}, u32[]{:S(2)}, u32[]{:S(2)}) collective-permute-start(f32[8,2048]{1,0:T(8,128)S(1)} %fusion.7), channel_id=1, source_target_pairs={{0,1},{1,2},{2,3},{3,4},{4,5},{5,6},{6,7},{7,0},{8,9},{9,10},{10,1... | collective-permute-start | bytes 196616 | tf_op jit(solution)/shard_map/ppermute | solution.py:29
  100.0 4.3 %collective-permute-start.15 = (f32[8,2048]{1,0:T(8,128)S(1)}, f32[8,2048]{1,0:T(8,128)S(1)}, u32[]{:S(2)}, u32[]{:S(2)}) collective-permute-start(f32[8,2048]{1,0:T(8,128)S(1)} %fusion.7), channel_id=1, source_target_pairs={{0,7},{1,0},{2,1},{3,2},{4,3},{5,4},{6,5},{7,6},{8,15},{9,8},{10,9... | collective-permute-start | bytes 196616 | tf_op jit(solution)/shard_map/ppermute | solution.py:29
  104.4 7.4 %collective-permute-start.16 = (f32[8,2048]{1,0:T(8,128)S(1)}, f32[8,2048]{1,0:T(8,128)S(1)}, u32[]{:S(2)}, u32[]{:S(2)}) collective-permute-start(f32[8,2048]{1,0:T(8,128)S(1)} %get-tuple-element.40), channel_id=1, source_target_pairs={{0,3},{1,4},{2,5},{3,6},{4,7},{5,0},{6,1},{7,2},{8,11},{9,12},{10,... | collective-permute-start | bytes 196616 | tf_op jit(solution)/shard_map/ppermute | solution.py:29
  104.6 7.3 %collective-permute-start.17 = (f32[8,2048]{1,0:T(8,128)S(1)}, f32[8,2048]{1,0:T(8,128)S(1)}, u32[]{:S(2)}, u32[]{:S(2)}) collective-permute-start(f32[8,2048]{1,0:T(8,128)S(1)} %get-tuple-element.41), channel_id=1, source_target_pairs={{0,5},{1,6},{2,7},{3,0},{4,1},{5,2},{6,3},{7,4},{8,13},{9,14},{10,... | collective-permute-start | bytes 196616 | tf_op jit(solution)/shard_map/ppermute | solution.py:29
  119.1 16.0 %collective-permute-start.18 = (bf16[256,512]{1,0:T(8,128)(2,1)S(1)}, bf16[256,512]{1,0:T(8,128)(2,1)S(1)}, u32[]{:S(2)}, u32[]{:S(2)}) collective-permute-start(bf16[256,512]{1,0:T(8,128)(2,1)S(1)} %get-tuple-element.48), channel_id=1, source_target_pairs={{0,8},{8,16},{16,24},{24,0},{1,9},{9,17},{17,25},{25,1},{2,10},{10... | collective-permute-start | bytes 786440 | tf_op jit(solution)/shard_map/ppermute | solution.py:29
  119.1 15.9 %collective-permute-start.19 = (bf16[256,512]{1,0:T(8,128)(2,1)S(1)}, bf16[256,512]{1,0:T(8,128)(2,1)S(1)}, u32[]{:S(2)}, u32[]{:S(2)}) collective-permute-start(bf16[256,512]{1,0:T(8,128)(2,1)S(1)} %get-tuple-element.47), channel_id=1, source_target_pairs={{0,24},{8,0},{16,8},{24,16},{1,25},{9,1},{17,9},{25,17},{2,26},{10... | collective-permute-start | bytes 786440 | tf_op jit(solution)/shard_map/ppermute | solution.py:29
  135.2 10.6 %copy-start.4 = (bf16[512,512]{1,0:T(8,128)(2,1)S(1)}, bf16[512,512]{1,0:T(8,128)(2,1)}, u32[]{:S(2)}) copy-start(bf16[512,512]{1,0:T(8,128)(2,1)} %copy-done.3) | copy-start | bytes 1572868
  142.5 10.5 %collective-permute-start.20 = (bf16[512,512]{1,0:T(8,128)(2,1)S(1)}, bf16[512,512]{1,0:T(8,128)(2,1)S(1)}, u32[]{:S(2)}, u32[]{:S(2)}) collective-permute-start(bf16[512,512]{1,0:T(8,128)(2,1)S(1)} %get-tuple-element.37), channel_id=1, source_target_pairs={{0,8},{8,16},{16,24},{24,0},{1,9},{9,17},{17,25},{25,1},{2,10},{10... | collective-permute-start | bytes 1572872 | tf_op jit(solution)/shard_map/ppermute | solution.py:29
  142.6 10.4 %collective-permute-start.21 = (bf16[512,512]{1,0:T(8,128)(2,1)S(1)}, bf16[512,512]{1,0:T(8,128)(2,1)S(1)}, u32[]{:S(2)}, u32[]{:S(2)}) collective-permute-start(bf16[512,512]{1,0:T(8,128)(2,1)S(1)} %get-tuple-element.38), channel_id=1, source_target_pairs={{0,24},{8,0},{16,8},{24,16},{1,25},{9,1},{17,9},{25,17},{2,26},{10... | collective-permute-start | bytes 1572872 | tf_op jit(solution)/shard_map/ppermute | solution.py:29
  150.6 11.7 %collective-permute-start.22 = (bf16[4,192,512]{2,1,0:T(8,128)(2,1)}, bf16[4,192,512]{2,1,0:T(8,128)(2,1)}, u32[]{:S(2)}, u32[]{:S(2)}) collective-permute-start(bf16[4,192,512]{2,1,0:T(8,128)(2,1)} %fusion), channel_id=1, source_target_pairs={{0,32},{32,0},{1,33},{33,1},{2,34},{34,2},{3,35},{35,3},{4,36},{36... | collective-permute-start | bytes 2359304 | tf_op jit(solution)/shard_map/ppermute | solution.py:328
  153.9 23.7 %all-to-all-start.1 = ((bf16[8,64,512]{2,1,0:T(8,128)(2,1)}), bf16[8,64,512]{2,1,0:T(8,128)(2,1)}, u32[]{:S(2)}, u32[]{:S(2)}) async-start(bf16[8,64,512]{2,1,0:T(8,128)(2,1)} %bitcast.35), calls=%async_computation.1 | async-start | bytes 1048576 | tf_op jit(solution)/shard_map/all_to_all | solution.py:338
  164.9 8.8 %collective-permute-start.23 = (bf16[192,512]{1,0:T(8,128)(2,1)S(1)}, bf16[192,512]{1,0:T(8,128)(2,1)S(1)}, u32[]{:S(2)}, u32[]{:S(2)}) collective-permute-start(bf16[192,512]{1,0:T(8,128)(2,1)S(1)} %get-tuple-element.44), channel_id=1, source_target_pairs={{0,64},{64,128},{128,192},{192,0},{1,65},{65,129},{129,193},{193,1... | collective-permute-start | bytes 589832 | tf_op jit(solution)/shard_map/ppermute | solution.py:29
  166.5 9.3 %collective-permute-start.24 = (bf16[192,512]{1,0:T(8,128)(2,1)S(1)}, bf16[192,512]{1,0:T(8,128)(2,1)S(1)}, u32[]{:S(2)}, u32[]{:S(2)}) collective-permute-start(bf16[192,512]{1,0:T(8,128)(2,1)S(1)} %get-tuple-element.46), channel_id=1, source_target_pairs={{0,128},{64,192},{128,0},{192,64},{1,129},{65,193},{129,1},{193,65... | collective-permute-start | bytes 589832 | tf_op jit(solution)/shard_map/ppermute | solution.py:29
  169.2 6.6 %collective-permute-start.25 = (bf16[192,512]{1,0:T(8,128)(2,1)S(1)}, bf16[192,512]{1,0:T(8,128)(2,1)S(1)}, u32[]{:S(2)}, u32[]{:S(2)}) collective-permute-start(bf16[192,512]{1,0:T(8,128)(2,1)S(1)} %get-tuple-element.45), channel_id=1, source_target_pairs={{0,192},{64,0},{128,64},{192,128},{1,193},{65,1},{129,65},{193,129... | collective-permute-start | bytes 589832 | tf_op jit(solution)/shard_map/ppermute | solution.py:29
  (9 other events, 53.2 us)

commit v3 on v2

--- a/solution.py
+++ b/solution.py
@@ -92,8 +92,9 @@
     )(*args)
 
 
-def rank_body(score_ref, anchor_ref, stat_ref):
+def rank_body(score_ref, three_ref, low_ref, high_ref, stat_ref, anchor_ref):
     rows, lanes = score_ref.shape
+    anchor_ref[...] = three_ref[...] + low_ref[...] + high_ref[...]
     members = anchor_ref.shape[0]
     groups = CHUNK // 8
     for lane in range(0, lanes, 128):
@@ -119,29 +120,37 @@
 
 def rank_sums(scores, anchors):
     rows, count = scores.shape
-    members = anchors.shape[0]
+    members = anchors[0].shape[0]
+    row_spec = pl.BlockSpec((members, TILE), lambda i: (0, i))
     return pl.pallas_call(
         rank_body,
         grid=(count // TILE,),
         in_specs=[
             pl.BlockSpec((rows, TILE), lambda i: (0, i)),
-            pl.BlockSpec((members, TILE), lambda i: (0, i)),
-        ],
-        out_specs=pl.BlockSpec((2 * members, TILE), lambda i: (0, i)),
-        out_shape=jax.ShapeDtypeStruct((2 * members, count), F32),
+            row_spec,
+            row_spec,
+            row_spec,
+        ],
+        out_specs=[pl.BlockSpec((2 * members, TILE), lambda i: (0, i)), row_spec],
+        out_shape=[
+            jax.ShapeDtypeStruct((2 * members, count), F32),
+            jax.ShapeDtypeStruct((members, count), F32),
+        ],
         cost_estimate=priced(12),
         compiler_params=pltpu.CompilerParams(vmem_limit_bytes=8 * 2**20),
         name="rank_sums",
-    )(scores, anchors)
+    )(scores, *anchors)
 
 
 def weight_body(*refs):
-    cut_ref, score_ref, anchor_ref, index_ref, stat_ref, gallery_ref, dscore_ref, query_ref, coef_ref = refs[-9:]
+    cut_ref, score_ref, anchor_ref, index_ref, three_ref, low_ref, high_ref, gallery_ref = refs[-11:-3]
+    dscore_ref, query_ref, coef_ref = refs[-3:]
+    stats = three_ref[...] + low_ref[...] + high_ref[...]
     rows, lanes = score_ref.shape
     members = anchor_ref.shape[0]
     cuts = cut_ref.shape[0]
-    rank = 0.5 + stat_ref[0:members, :]
-    slope = stat_ref[members : 2 * members, :] / TEMP
+    rank = 0.5 + stats[0:members]
+    slope = stats[members : 2 * members] / TEMP
     weight = jnp.zeros((members, lanes), F32)
     for c in range(cuts):
         cut = cut_ref[c].astype(F32)
@@ -187,10 +196,10 @@
         pl.BlockSpec((rows, TILE), here),
         pl.BlockSpec((members, TILE), here),
         pl.BlockSpec((members, TILE), here),
-        pl.BlockSpec((2 * members, TILE), here),
+        *[pl.BlockSpec((2 * members, TILE), here)] * 3,
         pl.BlockSpec((width, rows), lambda i: (0, 0)),
     ]
-    args = [cutoffs, scores, anchors, index, stats, turned]
+    args = [cutoffs, scores, anchors, index, *stats, turned]
     aliases = {}
     if dscore is not None:
         in_specs = [pl.BlockSpec(memory_space=pl.ANY), *in_specs]
@@ -272,7 +281,7 @@
     upper = shift(value, "z", -1)
     two = value + lower
     three = two + upper
-    return three + shift(three, "z", 3) + shift(two, "z", -3)
+    return three, shift(three, "z", 3), shift(two, "z", -3)
 
 
 def shard_terms(queries, gallery, positives, cutoffs):
@@ -303,8 +312,8 @@
     scores, anchors = carried
     stored = pltpu.with_memory_space_constraint(scores, pltpu.MemorySpace.HBM)
     scores = near(scores)
-    anchors = summed_over_gallery(anchors)
-    stats = summed_over_gallery(rank_sums(scores, anchors))
+    stats, anchors = rank_sums(scores, summed_over_gallery(anchors))
+    stats = summed_over_gallery(stats)
 
     weights = functools.partial(weight_blocks, cutoffs, stored, anchors, local, stats, gallery.T)
     dscore, part_far = weights(None, (2,), ny, BF16)

time: 181 us -> 182 us (level)
  transfers between devices with their start and end apart: 28 -> 28, of which waited for: 19 -> 18; matrix products, arithmetic and copies ran while one was open for 4% -> 4% of each run, Pallas kernels for 14% -> 17%
where the time goes in v3:
time: 182 us; the launch traced here: 179 us
  starting transfers between devices  60 us (33%)
  waiting for transfers between devices  53.1 us (29%)
  Pallas kernels  52.1 us (29%)
  other arithmetic  6.9 us (4%)
  local copies, waits for them, and re-layouts  6.25 us (3%)
    ppermute x25, starting transfers between devices, shift(): lax.ppermute(value, axis, [(i, (i + step) % peers) for i in range(peers)])  43.4 us
    ppermute x25, waiting for transfers between devices, shift(): lax.ppermute(value, axis, [(i, (i + step) % peers) for i in range(peers)])  40.1 us
    pallas_call x3, Pallas kernels, weight_blocks(): pl.pallas_call(weight_body, grid=(steps * len(which),), in_specs=in_specs...  26.8 us
    all_to_all x1, waiting for transfers between devices, shard_terms(): own = lax.all_to_all(copies, 'z', 0, 0, tiled=True).reshape(size, width)  13 us
    pallas_call x1, Pallas kernels, rank_sums(): pl.pallas_call(rank_body, grid=(count // TILE,), in_specs=[pl.BlockSpec((...  11 us
    pallas_call x4, Pallas kernels, score_block(): pl.pallas_call(score_body, grid=(steps,), in_specs=in_specs, out_specs=[p...  10.4 us
    all_to_all x1, starting transfers between devices, shard_terms(): lax.all_to_all(query_part.reshape(nz, size // nz, width), 'z', 0, 0, tile...  8.41 us
    all_to_all x1, starting transfers between devices, shard_terms(): own = lax.all_to_all(copies, 'z', 0, 0, tiled=True).reshape(size, width)  8.11 us
  transfers between devices with their start and end apart: 28, of which 18 were waited for; matrix products, arithmetic and copies ran while one was open for 4% of the time, Pallas kernels for 17%

profile of v3, /device:TPU:64, one launch (start us, length us, event | category | flops | bytes accessed | tf_op | source)
XLA Modules:
  0.0 179.3 jit_solution(14636473101191084385)
XLA Ops:
  2.3 8.1 %all-to-all-start = ((bf16[8,64,512]{2,1,0:T(8,128)(2,1)}), bf16[8,64,512]{2,1,0:T(8,128)(2,1)S(1)}, u32[]{:S(2)}, u32[]{:S(2)}) async-start(bf16[8,64,512]{2,1,0:T(8,128)(2,1)} %broadcast_in_dim.2), calls=%async_computation | async-start | bytes 1048576 | tf_op jit(solution)/shard_map/all_to_all | solution.py:299
  11.2 13.0 %all-to-all-done = bf16[8,64,512]{2,1,0:T(8,128)(2,1)S(1)} async-done(((bf16[8,64,512]{2,1,0:T(8,128)(2,1)}), bf16[8,64,512]{2,1,0:T(8,128)(2,1)S(1)}, u32[]{:S(2)}, u32[]{:S(2)}) %all-to-all-start) | async-done | bytes 524320 | tf_op jit(solution)/shard_map/all_to_all | solution.py:299
  24.2 3.0 %collective-permute-start = (bf16[512,512]{1,0:T(8,128)(2,1)S(1)}, bf16[512,512]{1,0:T(8,128)(2,1)S(1)}, u32[]{:S(2)}, u32[]{:S(2)}) collective-permute-start(bf16[512,512]{1,0:T(8,128)(2,1)S(1)} %bitcast.31), channel_id=1, source_target_pairs={{0,24},{8,0},{16,8},{24,16},{1,25},{9,1},{17,9},{25,17},{2,26},{10... | collective-permute-start | bytes 1572872 | tf_op jit(solution)/shard_map/ppermute | solution.py:29
  28.7 2.6 %shard_map.59 = (f32[1536,2048]{1,0:T(8,128)S(1)}, f32[4,2048]{1,0:T(4,128)S(1)}) custom-call(bf16[1536,512]{1,0:T(8,128)(2,1)S(1)} %copy-done.1, bf16[512,512]{1,0:T(8,128)(2,1)S(1)} %bitcast.33, s32[4,512]{1,0:T(4,128)S(1)} %get-tuple-element.60.refs_2_), custom_call_target="tpu_custom_call" | custom-call | flops 2500000000 | bytes 5000000 | tf_op jit(solution)/shard_map/pallas_call | solution.py:77
  31.3 6.1 %collective-permute-done.refs_3_.refs_1_ = bf16[512,512]{1,0:T(8,128)(2,1)S(1)} collective-permute-done((bf16[512,512]{1,0:T(8,128)(2,1)S(1)}, bf16[512,512]{1,0:T(8,128)(2,1)S(1)}, u32[]{:S(2)}, u32[]{:S(2)}) %collective-permute-start) | collective-permute-done | bytes 524320 | tf_op jit(solution)/shard_map/ppermute | solution.py:29
  37.4 3.8 %collective-permute-start.2 = (bf16[256,512]{1,0:T(8,128)(2,1)S(1)}, bf16[256,512]{1,0:T(8,128)(2,1)S(1)}, u32[]{:S(2)}, u32[]{:S(2)}) collective-permute-start(bf16[256,512]{1,0:T(8,128)(2,1)S(1)} %slice.95), channel_id=1, source_target_pairs={{0,24},{8,0},{16,8},{24,16},{1,25},{9,1},{17,9},{25,17},{2,26},{10... | collective-permute-start | bytes 786440 | tf_op jit(solution)/shard_map/ppermute | solution.py:29
  41.3 2.6 %shard_map.60 = (f32[1536,2048]{1,0:T(8,128)S(1)}, f32[4,2048]{1,0:T(4,128)S(1)}) custom-call(f32[1536,2048]{1,0:T(8,128)S(1)} %get-tuple-element.23.refs_0_, f32[4,2048]{1,0:T(4,128)S(1)} %get-tuple-element.24.refs_1_, bf16[1536,512]{1,0:T(8,128)(2,1)S(1)} %copy-done.1, ...), custom_call_target="tpu_custom_call", output_to_operand_aliasing={{0}: (0, {}), {1}: (1, {})} | custom-call | flops 2500000000 | bytes 5000000 | tf_op jit(solution)/shard_map/pallas_call | solution.py:77
  44.0 2.6 %shard_map.61 = (f32[1536,2048]{1,0:T(8,128)S(1)}, f32[4,2048]{1,0:T(4,128)S(1)}) custom-call(f32[1536,2048]{1,0:T(8,128)S(1)} %get-tuple-element.25.refs_0_, f32[4,2048]{1,0:T(4,128)S(1)} %get-tuple-element.26.refs_1_, bf16[1536,512]{1,0:T(8,128)(2,1)S(1)} %copy-done.1, ...), custom_call_target="tpu_custom_call", output_to_operand_aliasing={{0}: (0, {}), {1}: (1, {})} | custom-call | flops 2500000000 | bytes 5000000 | tf_op jit(solution)/shard_map/pallas_call | solution.py:77
  46.6 2.3 %collective-permute-done.3 = bf16[256,512]{1,0:T(8,128)(2,1)S(1)} collective-permute-done((bf16[256,512]{1,0:T(8,128)(2,1)S(1)}, bf16[256,512]{1,0:T(8,128)(2,1)S(1)}, u32[]{:S(2)}, u32[]{:S(2)}) %collective-permute-start.3) | collective-permute-done | bytes 262176 | tf_op jit(solution)/shard_map/ppermute | solution.py:29
  48.9 2.6 %shard_map.62 = (f32[1536,2048]{1,0:T(8,128)S(1)}, f32[4,2048]{1,0:T(4,128)S(1)}) custom-call(f32[1536,2048]{1,0:T(8,128)S(1)} %get-tuple-element.27.refs_0_, f32[4,2048]{1,0:T(4,128)S(1)} %get-tuple-element.28.refs_1_, bf16[1536,512]{1,0:T(8,128)(2,1)S(1)} %copy-done.1, ...), custom_call_target="tpu_custom_call", output_to_operand_aliasing={{0}: (0, {}), {1}: (1, {})} | custom-call | flops 2500000000 | bytes 5000000 | tf_op jit(solution)/shard_map/pallas_call | solution.py:77
  55.6 2.1 %collective-permute-done.4 = f32[4,2048]{1,0:T(4,128)S(1)} collective-permute-done((f32[4,2048]{1,0:T(4,128)S(1)}, f32[4,2048]{1,0:T(4,128)S(1)}, u32[]{:S(2)}, u32[]{:S(2)}) %collective-permute-start.4) | collective-permute-done | bytes 32800 | tf_op jit(solution)/shard_map/ppermute | solution.py:29
  61.2 1.9 %collective-permute-done.7 = f32[4,2048]{1,0:T(4,128)S(1)} collective-permute-done((f32[4,2048]{1,0:T(4,128)S(1)}, f32[4,2048]{1,0:T(4,128)S(1)}, u32[]{:S(2)}, u32[]{:S(2)}) %collective-permute-start.7) | collective-permute-done | bytes 32800 | tf_op jit(solution)/shard_map/ppermute | solution.py:29
  63.9 8.8 %collective-permute-start.10 = (f32[4,2048]{1,0:T(4,128)S(1)}, f32[4,2048]{1,0:T(4,128)S(1)}, u32[]{:S(2)}, u32[]{:S(2)}) collective-permute-start(f32[4,2048]{1,0:T(4,128)S(1)} %get-tuple-element.47), channel_id=1, source_target_pairs={{0,5},{1,6},{2,7},{3,0},{4,1},{5,2},{6,3},{7,4},{8,13},{9,14},{10,... | collective-permute-start | bytes 98312 | tf_op jit(solution)/shard_map/ppermute | solution.py:29
  74.3 5.3 %collective-permute-done.9.low_ref = f32[4,2048]{1,0:T(4,128)S(1)} collective-permute-done((f32[4,2048]{1,0:T(4,128)S(1)}, f32[4,2048]{1,0:T(4,128)S(1)}, u32[]{:S(2)}, u32[]{:S(2)}) %collective-permute-start.9) | collective-permute-done | bytes 32800 | tf_op jit(solution)/shard_map/ppermute | solution.py:29
  79.6 11.0 %rank_sums.1 = (f32[8,2048]{1,0:T(8,128)S(1)}, f32[4,2048]{1,0:T(4,128)S(1)}) custom-call(f32[1536,2048]{1,0:T(8,128)S(1)} %get-tuple-element.29.score_ref.refs_1_.refs_2_, f32[4,2048]{1,0:T(4,128)S(1)} %get-tuple-element.46.three_ref, f32[4,2048]{1,0:T(4,128)S(1)} %collective-permute-done.9.low_ref, f32[4,2048]{1,0:T(4,128)S(1)} %collective-permute-done.10.high_ref), custom_call_target="tpu_custom_call" | custom-call | flops 6000000000 | bytes 12000000 | tf_op jit(solution)/shard_map/rank_sums/pallas_call | solution.py:125
  90.9 3.2 %collective-permute-start.13 = (f32[8,2048]{1,0:T(8,128)S(1)}, f32[8,2048]{1,0:T(8,128)S(1)}, u32[]{:S(2)}, u32[]{:S(2)}) collective-permute-start(f32[8,2048]{1,0:T(8,128)S(1)} %get-tuple-element.32), channel_id=1, source_target_pairs={{0,24},{8,0},{16,8},{24,16},{1,25},{9,1},{17,9},{25,17},{2,26},{10... | collective-permute-start | bytes 196616 | tf_op jit(solution)/shard_map/ppermute | solution.py:29
  94.2 2.2 %collective-permute-done.11 = f32[8,2048]{1,0:T(8,128)S(1)} collective-permute-done((f32[8,2048]{1,0:T(8,128)S(1)}, f32[8,2048]{1,0:T(8,128)S(1)}, u32[]{:S(2)}, u32[]{:S(2)}) %collective-permute-start.11) | collective-permute-done | bytes 65568 | tf_op jit(solution)/shard_map/ppermute | solution.py:29
  96.4 3.5 %collective-permute-done.12 = f32[8,2048]{1,0:T(8,128)S(1)} collective-permute-done((f32[8,2048]{1,0:T(8,128)S(1)}, f32[8,2048]{1,0:T(8,128)S(1)}, u32[]{:S(2)}, u32[]{:S(2)}) %collective-permute-start.12) | collective-permute-done | bytes 65568 | tf_op jit(solution)/shard_map/ppermute | solution.py:29
  100.1 2.0 %collective-permute-start.15 = (f32[8,2048]{1,0:T(8,128)S(1)}, f32[8,2048]{1,0:T(8,128)S(1)}, u32[]{:S(2)}, u32[]{:S(2)}) collective-permute-start(f32[8,2048]{1,0:T(8,128)S(1)} %fusion.7), channel_id=1, source_target_pairs={{0,7},{1,0},{2,1},{3,2},{4,3},{5,4},{6,5},{7,6},{8,15},{9,8},{10,9... | collective-permute-start | bytes 196616 | tf_op jit(solution)/shard_map/ppermute | solution.py:29
  102.1 2.2 %collective-permute-done.14 = f32[8,2048]{1,0:T(8,128)S(1)} collective-permute-done((f32[8,2048]{1,0:T(8,128)S(1)}, f32[8,2048]{1,0:T(8,128)S(1)}, u32[]{:S(2)}, u32[]{:S(2)}) %collective-permute-start.14) | collective-permute-done | bytes 65568 | tf_op jit(solution)/shard_map/ppermute | solution.py:29
  104.6 4.9 %collective-permute-start.17 = (f32[8,2048]{1,0:T(8,128)S(1)}, f32[8,2048]{1,0:T(8,128)S(1)}, u32[]{:S(2)}, u32[]{:S(2)}) collective-permute-start(f32[8,2048]{1,0:T(8,128)S(1)} %get-tuple-element.45), channel_id=1, source_target_pairs={{0,5},{1,6},{2,7},{3,0},{4,1},{5,2},{6,3},{7,4},{8,13},{9,14},{10,... | collective-permute-start | bytes 196616 | tf_op jit(solution)/shard_map/ppermute | solution.py:29
  111.9 7.0 %shard_map.63 = (bf16[1536,2048]{1,0:T(8,128)(2,1)S(1)}, bf16[512,512]{1,0:T(8,128)(2,1)S(1)}) custom-call(s32[4]{0:T(128)S(1)} %copy-done.11, f32[1536,2048]{1,0:T(8,128)} %copy-done, f32[4,2048]{1,0:T(4,128)S(1)} %get-tuple-element.31.refs_2_.refs_3_, s32[4,2048]{1,0:T(4,128)S(1)} %fusion.8.refs_3_.refs_4_, ...), custom_call_target="tpu_custom_call" | custom-call | flops 3000000000 | bytes 6000000 | tf_op jit(solution)/shard_map/pallas_call | solution.py:208
  119.1 3.2 %collective-permute-start.19 = (bf16[256,512]{1,0:T(8,128)(2,1)S(1)}, bf16[256,512]{1,0:T(8,128)(2,1)S(1)}, u32[]{:S(2)}, u32[]{:S(2)}) collective-permute-start(bf16[256,512]{1,0:T(8,128)(2,1)S(1)} %get-tuple-element.51), channel_id=1, source_target_pairs={{0,24},{8,0},{16,8},{24,16},{1,25},{9,1},{17,9},{25,17},{2,26},{10... | collective-permute-start | bytes 786440 | tf_op jit(solution)/shard_map/ppermute | solution.py:29
  122.3 12.7 %shard_map.64 = (bf16[1536,2048]{1,0:T(8,128)(2,1)S(1)}, f32[1024,512]{1,0:T(8,128)S(1)}) custom-call(bf16[1536,2048]{1,0:T(8,128)(2,1)S(1)} %get-tuple-element.33.refs_0_, s32[4]{0:T(128)S(1)} %copy-done.11, f32[1536,2048]{1,0:T(8,128)} %copy-done, f32[4,2048]{1,0:T(4,128)S(1)} %get-tuple-element.31.refs_2_.refs_3_, ...), custom_call_target="tpu_custom_call", output_to_operand_aliasing={{0}: (0, {})} | custom-call | flops 6000000000 | bytes 12000000 | tf_op jit(solution)/shard_map/pallas_call | solution.py:208
  135.3 3.2 %collective-permute-start.21 = (bf16[512,512]{1,0:T(8,128)(2,1)S(1)}, bf16[512,512]{1,0:T(8,128)(2,1)S(1)}, u32[]{:S(2)}, u32[]{:S(2)}) collective-permute-start(bf16[512,512]{1,0:T(8,128)(2,1)S(1)} %get-tuple-element.42), channel_id=1, source_target_pairs={{0,24},{8,0},{16,8},{24,16},{1,25},{9,1},{17,9},{25,17},{2,26},{10... | collective-permute-start | bytes 1572872 | tf_op jit(solution)/shard_map/ppermute | solution.py:29
  138.6 7.0 %shard_map.65 = (bf16[1536,2048]{1,0:T(8,128)(2,1)S(1)}, f32[512,512]{1,0:T(8,128)S(1)}) custom-call(bf16[1536,2048]{1,0:T(8,128)(2,1)S(1)} %get-tuple-element.39.refs_0_, s32[4]{0:T(128)S(1)} %copy-done.11, f32[1536,2048]{1,0:T(8,128)} %copy-done, f32[4,2048]{1,0:T(4,128)S(1)} %get-tuple-element.31.refs_2_.refs_3_, ...), custom_call_target="tpu_custom_call", output_to_operand_aliasing={{0}: (0, {})} | custom-call | flops 3000000000 | bytes 6000000 | tf_op jit(solution)/shard_map/pallas_call | solution.py:208
  145.6 3.8 %gallery_terms.1 = f32[1536,512]{1,0:T(8,128)S(1)} custom-call(bf16[1536,2048]{1,0:T(8,128)(2,1)S(1)} %get-tuple-element.43.dscore_ref, bf16[512,512]{1,0:T(8,128)(2,1)S(1)} %bitcast.34, bf16[512,512]{1,0:T(8,128)(2,1)S(1)} %copy-done.4, bf16[512,512]{1,0:T(8,128)(2,1)S(1)} %copy-done.8, bf16[512,512]{1,0:T(8,128)(2,1)S(1)} %copy-done.6), custom_call_target="tpu_custom_call" | custom-call | flops 3000000000 | bytes 6000000 | tf_op jit(solution)/shard_map/gallery_terms/pallas_call | solution.py:260
  151.4 8.4 %all-to-all-start.1 = ((bf16[8,64,512]{2,1,0:T(8,128)(2,1)}), bf16[8,64,512]{2,1,0:T(8,128)(2,1)}, u32[]{:S(2)}, u32[]{:S(2)}) async-start(bf16[8,64,512]{2,1,0:T(8,128)(2,1)} %bitcast.35), calls=%async_computation.1 | async-start | bytes 1048576 | tf_op jit(solution)/shard_map/all_to_all | solution.py:347
  164.1 2.7 %collective-permute-start.24 = (bf16[192,512]{1,0:T(8,128)(2,1)S(1)}, bf16[192,512]{1,0:T(8,128)(2,1)S(1)}, u32[]{:S(2)}, u32[]{:S(2)}) collective-permute-start(bf16[192,512]{1,0:T(8,128)(2,1)S(1)} %get-tuple-element.50), channel_id=1, source_target_pairs={{0,128},{64,192},{128,0},{192,64},{1,129},{65,193},{129,1},{193,65... | collective-permute-start | bytes 589832 | tf_op jit(solution)/shard_map/ppermute | solution.py:29
  168.2 2.4 %collective-permute-done.23 = bf16[192,512]{1,0:T(8,128)(2,1)S(1)} collective-permute-done((bf16[192,512]{1,0:T(8,128)(2,1)S(1)}, bf16[192,512]{1,0:T(8,128)(2,1)S(1)}, u32[]{:S(2)}, u32[]{:S(2)}) %collective-permute-start.23) | collective-permute-done | bytes 196640 | tf_op jit(solution)/shard_map/ppermute | solution.py:29
  170.6 5.1 %collective-permute-done.24 = bf16[192,512]{1,0:T(8,128)(2,1)S(1)} collective-permute-done((bf16[192,512]{1,0:T(8,128)(2,1)S(1)}, bf16[192,512]{1,0:T(8,128)(2,1)S(1)}, u32[]{:S(2)}, u32[]{:S(2)}) %collective-permute-start.24) | collective-permute-done | bytes 196640 | tf_op jit(solution)/shard_map/ppermute | solution.py:29
  175.7 1.8 %fusion.2 = f32[192,512]{1,0:T(8,128)} fusion(bf16[192,512]{1,0:T(8,128)(2,1)S(1)} %collective-permute-done.25, bf16[192,512]{1,0:T(8,128)(2,1)S(1)} %collective-permute-done.24, bf16[192,512]{1,0:T(8,128)(2,1)S(1)} %collective-permute-done.23, f32[4,192,512]{2,1,0:T(8,128)} %copy-done.12, s32[]{:T(128)S(6)} %select_n.41), kind=kLoop, calls=%fused_computation.7 | loop fusion | flops 589824 | bytes 1376260 | tf_op jit(solution)/shard_map/add | solution.py:344
  (90 shorter events, 26.9 us)
Async XLA Ops:
  2.3 21.9 %all-to-all-start = ((bf16[8,64,512]{2,1,0:T(8,128)(2,1)}), bf16[8,64,512]{2,1,0:T(8,128)(2,1)S(1)}, u32[]{:S(2)}, u32[]{:S(2)}) async-start(bf16[8,64,512]{2,1,0:T(8,128)(2,1)} %broadcast_in_dim.2), calls=%async_computation | async-start | bytes 1048576 | tf_op jit(solution)/shard_map/all_to_all | solution.py:299
  24.2 13.2 %collective-permute-start = (bf16[512,512]{1,0:T(8,128)(2,1)S(1)}, bf16[512,512]{1,0:T(8,128)(2,1)S(1)}, u32[]{:S(2)}, u32[]{:S(2)}) collective-permute-start(bf16[512,512]{1,0:T(8,128)(2,1)S(1)} %bitcast.31), channel_id=1, source_target_pairs={{0,24},{8,0},{16,8},{24,16},{1,25},{9,1},{17,9},{25,17},{2,26},{10... | collective-permute-start | bytes 1572872 | tf_op jit(solution)/shard_map/ppermute | solution.py:29
  27.2 14.0 %collective-permute-start.1 = (bf16[512,512]{1,0:T(8,128)(2,1)S(1)}, bf16[512,512]{1,0:T(8,128)(2,1)S(1)}, u32[]{:S(2)}, u32[]{:S(2)}) collective-permute-start(bf16[512,512]{1,0:T(8,128)(2,1)S(1)} %bitcast.32), channel_id=1, source_target_pairs={{0,8},{8,16},{16,24},{24,0},{1,9},{9,17},{17,25},{25,1},{2,10},{10... | collective-permute-start | bytes 1572872 | tf_op jit(solution)/shard_map/ppermute | solution.py:29
  37.4 9.2 %collective-permute-start.2 = (bf16[256,512]{1,0:T(8,128)(2,1)S(1)}, bf16[256,512]{1,0:T(8,128)(2,1)S(1)}, u32[]{:S(2)}, u32[]{:S(2)}) collective-permute-start(bf16[256,512]{1,0:T(8,128)(2,1)S(1)} %slice.95), channel_id=1, source_target_pairs={{0,24},{8,0},{16,8},{24,16},{1,25},{9,1},{17,9},{25,17},{2,26},{10... | collective-permute-start | bytes 786440 | tf_op jit(solution)/shard_map/ppermute | solution.py:29
  41.2 7.7 %collective-permute-start.3 = (bf16[256,512]{1,0:T(8,128)(2,1)S(1)}, bf16[256,512]{1,0:T(8,128)(2,1)S(1)}, u32[]{:S(2)}, u32[]{:S(2)}) collective-permute-start(bf16[256,512]{1,0:T(8,128)(2,1)S(1)} %slice.96), channel_id=1, source_target_pairs={{0,8},{8,16},{16,24},{24,0},{1,9},{9,17},{17,25},{25,1},{2,10},{10... | collective-permute-start | bytes 786440 | tf_op jit(solution)/shard_map/ppermute | solution.py:29
  51.5 39.1 %copy-start = (f32[1536,2048]{1,0:T(8,128)}, f32[1536,2048]{1,0:T(8,128)S(1)}, u32[]{:S(2)}) copy-start(f32[1536,2048]{1,0:T(8,128)S(1)} %get-tuple-element.29.score_ref.refs_1_.refs_2_) | copy-start | bytes 37748740
  51.6 4.0 %collective-permute-start.6 = (f32[4,2048]{1,0:T(4,128)S(1)}, f32[4,2048]{1,0:T(4,128)S(1)}, u32[]{:S(2)}, u32[]{:S(2)}) collective-permute-start(f32[4,2048]{1,0:T(4,128)S(1)} %get-tuple-element.30), channel_id=1, source_target_pairs={{0,24},{8,0},{16,8},{24,16},{1,25},{9,1},{17,9},{25,17},{2,26},{10... | collective-permute-start | bytes 98312 | tf_op jit(solution)/shard_map/ppermute | solution.py:29
  52.6 5.1 %collective-permute-start.4 = (f32[4,2048]{1,0:T(4,128)S(1)}, f32[4,2048]{1,0:T(4,128)S(1)}, u32[]{:S(2)}, u32[]{:S(2)}) collective-permute-start(f32[4,2048]{1,0:T(4,128)S(1)} %get-tuple-element.30), channel_id=1, source_target_pairs={{0,8},{8,16},{16,24},{24,0},{1,9},{9,17},{17,25},{25,1},{2,10},{10... | collective-permute-start | bytes 98312 | tf_op jit(solution)/shard_map/ppermute | solution.py:29
  53.7 5.4 %collective-permute-start.5 = (f32[4,2048]{1,0:T(4,128)S(1)}, f32[4,2048]{1,0:T(4,128)S(1)}, u32[]{:S(2)}, u32[]{:S(2)}) collective-permute-start(f32[4,2048]{1,0:T(4,128)S(1)} %get-tuple-element.30), channel_id=1, source_target_pairs={{0,16},{8,24},{16,0},{24,8},{1,17},{9,25},{17,1},{25,9},{2,18},{10... | collective-permute-start | bytes 98312 | tf_op jit(solution)/shard_map/ppermute | solution.py:29
  59.1 4.0 %collective-permute-start.7 = (f32[4,2048]{1,0:T(4,128)S(1)}, f32[4,2048]{1,0:T(4,128)S(1)}, u32[]{:S(2)}, u32[]{:S(2)}) collective-permute-start(f32[4,2048]{1,0:T(4,128)S(1)} %fusion.10), channel_id=1, source_target_pairs={{0,1},{1,2},{2,3},{3,4},{4,5},{5,6},{6,7},{7,0},{8,9},{9,10},{10,1... | collective-permute-start | bytes 98312 | tf_op jit(solution)/shard_map/ppermute | solution.py:29
  59.9 3.9 %collective-permute-start.8 = (f32[4,2048]{1,0:T(4,128)S(1)}, f32[4,2048]{1,0:T(4,128)S(1)}, u32[]{:S(2)}, u32[]{:S(2)}) collective-permute-start(f32[4,2048]{1,0:T(4,128)S(1)} %fusion.10), channel_id=1, source_target_pairs={{0,7},{1,0},{2,1},{3,2},{4,3},{5,4},{6,5},{7,6},{8,15},{9,8},{10,9... | collective-permute-start | bytes 98312 | tf_op jit(solution)/shard_map/ppermute | solution.py:29
  63.9 10.4 %collective-permute-start.10 = (f32[4,2048]{1,0:T(4,128)S(1)}, f32[4,2048]{1,0:T(4,128)S(1)}, u32[]{:S(2)}, u32[]{:S(2)}) collective-permute-start(f32[4,2048]{1,0:T(4,128)S(1)} %get-tuple-element.47), channel_id=1, source_target_pairs={{0,5},{1,6},{2,7},{3,0},{4,1},{5,2},{6,3},{7,4},{8,13},{9,14},{10,... | collective-permute-start | bytes 98312 | tf_op jit(solution)/shard_map/ppermute | solution.py:29
  72.7 6.9 %collective-permute-start.9 = (f32[4,2048]{1,0:T(4,128)S(1)}, f32[4,2048]{1,0:T(4,128)S(1)}, u32[]{:S(2)}, u32[]{:S(2)}) collective-permute-start(f32[4,2048]{1,0:T(4,128)S(1)} %get-tuple-element.46.three_ref), channel_id=1, source_target_pairs={{0,3},{1,4},{2,5},{3,6},{4,7},{5,0},{6,1},{7,2},{8,11},{9,12},{10,... | collective-permute-start | bytes 98312 | tf_op jit(solution)/shard_map/ppermute | solution.py:29
  79.6 29.9 %copy-start.2 = (bf16[1536,512]{1,0:T(8,128)(2,1)S(1)}, bf16[1536,512]{1,0:T(8,128)(2,1)}, u32[]{:S(2)}) copy-start(bf16[1536,512]{1,0:T(8,128)(2,1)} %refs_2_.5) | copy-start | bytes 4718596
  90.7 21.3 %copy-start.11 = (s32[4]{0:T(128)S(1)}, s32[4]{0:T(128)}, u32[]{:S(2)}) copy-start(s32[4]{0:T(128)} %refs_1_.3) | copy-start | bytes 52
  90.7 5.7 %collective-permute-start.11 = (f32[8,2048]{1,0:T(8,128)S(1)}, f32[8,2048]{1,0:T(8,128)S(1)}, u32[]{:S(2)}, u32[]{:S(2)}) collective-permute-start(f32[8,2048]{1,0:T(8,128)S(1)} %get-tuple-element.32), channel_id=1, source_target_pairs={{0,8},{8,16},{16,24},{24,0},{1,9},{9,17},{17,25},{25,1},{2,10},{10... | collective-permute-start | bytes 196616 | tf_op jit(solution)/shard_map/ppermute | solution.py:29
  90.9 5.5 %collective-permute-start.13 = (f32[8,2048]{1,0:T(8,128)S(1)}, f32[8,2048]{1,0:T(8,128)S(1)}, u32[]{:S(2)}, u32[]{:S(2)}) collective-permute-start(f32[8,2048]{1,0:T(8,128)S(1)} %get-tuple-element.32), channel_id=1, source_target_pairs={{0,24},{8,0},{16,8},{24,16},{1,25},{9,1},{17,9},{25,17},{2,26},{10... | collective-permute-start | bytes 196616 | tf_op jit(solution)/shard_map/ppermute | solution.py:29
  94.2 5.8 %collective-permute-start.12 = (f32[8,2048]{1,0:T(8,128)S(1)}, f32[8,2048]{1,0:T(8,128)S(1)}, u32[]{:S(2)}, u32[]{:S(2)}) collective-permute-start(f32[8,2048]{1,0:T(8,128)S(1)} %get-tuple-element.32), channel_id=1, source_target_pairs={{0,16},{8,24},{16,0},{24,8},{1,17},{9,25},{17,1},{25,9},{2,18},{10... | collective-permute-start | bytes 196616 | tf_op jit(solution)/shard_map/ppermute | solution.py:29
  100.0 4.3 %collective-permute-start.14 = (f32[8,2048]{1,0:T(8,128)S(1)}, f32[8,2048]{1,0:T(8,128)S(1)}, u32[]{:S(2)}, u32[]{:S(2)}) collective-permute-start(f32[8,2048]{1,0:T(8,128)S(1)} %fusion.7), channel_id=1, source_target_pairs={{0,1},{1,2},{2,3},{3,4},{4,5},{5,6},{6,7},{7,0},{8,9},{9,10},{10,1... | collective-permute-start | bytes 196616 | tf_op jit(solution)/shard_map/ppermute | solution.py:29
  100.1 4.3 %collective-permute-start.15 = (f32[8,2048]{1,0:T(8,128)S(1)}, f32[8,2048]{1,0:T(8,128)S(1)}, u32[]{:S(2)}, u32[]{:S(2)}) collective-permute-start(f32[8,2048]{1,0:T(8,128)S(1)} %fusion.7), channel_id=1, source_target_pairs={{0,7},{1,0},{2,1},{3,2},{4,3},{5,4},{6,5},{7,6},{8,15},{9,8},{10,9... | collective-permute-start | bytes 196616 | tf_op jit(solution)/shard_map/ppermute | solution.py:29
  104.4 7.4 %collective-permute-start.16 = (f32[8,2048]{1,0:T(8,128)S(1)}, f32[8,2048]{1,0:T(8,128)S(1)}, u32[]{:S(2)}, u32[]{:S(2)}) collective-permute-start(f32[8,2048]{1,0:T(8,128)S(1)} %get-tuple-element.44.refs_4_.refs_5_), channel_id=1, source_target_pairs={{0,3},{1,4},{2,5},{3,6},{4,7},{5,0},{6,1},{7,2},{8,11},{9,12},{10,... | collective-permute-start | bytes 196616 | tf_op jit(solution)/shard_map/ppermute | solution.py:29
  104.6 7.3 %collective-permute-start.17 = (f32[8,2048]{1,0:T(8,128)S(1)}, f32[8,2048]{1,0:T(8,128)S(1)}, u32[]{:S(2)}, u32[]{:S(2)}) collective-permute-start(f32[8,2048]{1,0:T(8,128)S(1)} %get-tuple-element.45), channel_id=1, source_target_pairs={{0,5},{1,6},{2,7},{3,0},{4,1},{5,2},{6,3},{7,4},{8,13},{9,14},{10,... | collective-permute-start | bytes 196616 | tf_op jit(solution)/shard_map/ppermute | solution.py:29
  119.0 16.0 %collective-permute-start.18 = (bf16[256,512]{1,0:T(8,128)(2,1)S(1)}, bf16[256,512]{1,0:T(8,128)(2,1)S(1)}, u32[]{:S(2)}, u32[]{:S(2)}) collective-permute-start(bf16[256,512]{1,0:T(8,128)(2,1)S(1)} %get-tuple-element.52), channel_id=1, source_target_pairs={{0,8},{8,16},{16,24},{24,0},{1,9},{9,17},{17,25},{25,1},{2,10},{10... | collective-permute-start | bytes 786440 | tf_op jit(solution)/shard_map/ppermute | solution.py:29
  119.1 15.9 %collective-permute-start.19 = (bf16[256,512]{1,0:T(8,128)(2,1)S(1)}, bf16[256,512]{1,0:T(8,128)(2,1)S(1)}, u32[]{:S(2)}, u32[]{:S(2)}) collective-permute-start(bf16[256,512]{1,0:T(8,128)(2,1)S(1)} %get-tuple-element.51), channel_id=1, source_target_pairs={{0,24},{8,0},{16,8},{24,16},{1,25},{9,1},{17,9},{25,17},{2,26},{10... | collective-permute-start | bytes 786440 | tf_op jit(solution)/shard_map/ppermute | solution.py:29
  135.2 10.4 %copy-start.4 = (bf16[512,512]{1,0:T(8,128)(2,1)S(1)}, bf16[512,512]{1,0:T(8,128)(2,1)}, u32[]{:S(2)}) copy-start(bf16[512,512]{1,0:T(8,128)(2,1)} %copy-done.3) | copy-start | bytes 1572868
  135.2 15.2 %collective-permute-start.20 = (bf16[512,512]{1,0:T(8,128)(2,1)S(1)}, bf16[512,512]{1,0:T(8,128)(2,1)S(1)}, u32[]{:S(2)}, u32[]{:S(2)}) collective-permute-start(bf16[512,512]{1,0:T(8,128)(2,1)S(1)} %get-tuple-element.41), channel_id=1, source_target_pairs={{0,8},{8,16},{16,24},{24,0},{1,9},{9,17},{17,25},{25,1},{2,10},{10... | collective-permute-start | bytes 1572872 | tf_op jit(solution)/shard_map/ppermute | solution.py:29
  135.3 15.1 %collective-permute-start.21 = (bf16[512,512]{1,0:T(8,128)(2,1)S(1)}, bf16[512,512]{1,0:T(8,128)(2,1)S(1)}, u32[]{:S(2)}, u32[]{:S(2)}) collective-permute-start(bf16[512,512]{1,0:T(8,128)(2,1)S(1)} %get-tuple-element.42), channel_id=1, source_target_pairs={{0,24},{8,0},{16,8},{24,16},{1,25},{9,1},{17,9},{25,17},{2,26},{10... | collective-permute-start | bytes 1572872 | tf_op jit(solution)/shard_map/ppermute | solution.py:29
  150.4 9.4 %collective-permute-start.22 = (bf16[4,192,512]{2,1,0:T(8,128)(2,1)}, bf16[4,192,512]{2,1,0:T(8,128)(2,1)}, u32[]{:S(2)}, u32[]{:S(2)}) collective-permute-start(bf16[4,192,512]{2,1,0:T(8,128)(2,1)} %fusion), channel_id=1, source_target_pairs={{0,32},{32,0},{1,33},{33,1},{2,34},{34,2},{3,35},{35,3},{4,36},{36... | collective-permute-start | bytes 2359304 | tf_op jit(solution)/shard_map/ppermute | solution.py:337
  151.4 26.1 %all-to-all-start.1 = ((bf16[8,64,512]{2,1,0:T(8,128)(2,1)}), bf16[8,64,512]{2,1,0:T(8,128)(2,1)}, u32[]{:S(2)}, u32[]{:S(2)}) async-start(bf16[8,64,512]{2,1,0:T(8,128)(2,1)} %bitcast.35), calls=%async_computation.1 | async-start | bytes 1048576 | tf_op jit(solution)/shard_map/all_to_all | solution.py:347
  162.5 8.1 %collective-permute-start.23 = (bf16[192,512]{1,0:T(8,128)(2,1)S(1)}, bf16[192,512]{1,0:T(8,128)(2,1)S(1)}, u32[]{:S(2)}, u32[]{:S(2)}) collective-permute-start(bf16[192,512]{1,0:T(8,128)(2,1)S(1)} %get-tuple-element.48), channel_id=1, source_target_pairs={{0,64},{64,128},{128,192},{192,0},{1,65},{65,129},{129,193},{193,1... | collective-permute-start | bytes 589832 | tf_op jit(solution)/shard_map/ppermute | solution.py:29
  164.1 11.6 %collective-permute-start.24 = (bf16[192,512]{1,0:T(8,128)(2,1)S(1)}, bf16[192,512]{1,0:T(8,128)(2,1)S(1)}, u32[]{:S(2)}, u32[]{:S(2)}) collective-permute-start(bf16[192,512]{1,0:T(8,128)(2,1)S(1)} %get-tuple-element.50), channel_id=1, source_target_pairs={{0,128},{64,192},{128,0},{192,64},{1,129},{65,193},{129,1},{193,65... | collective-permute-start | bytes 589832 | tf_op jit(solution)/shard_map/ppermute | solution.py:29
  166.8 8.9 %collective-permute-start.25 = (bf16[192,512]{1,0:T(8,128)(2,1)S(1)}, bf16[192,512]{1,0:T(8,128)(2,1)S(1)}, u32[]{:S(2)}, u32[]{:S(2)}) collective-permute-start(bf16[192,512]{1,0:T(8,128)(2,1)S(1)} %get-tuple-element.49), channel_id=1, source_target_pairs={{0,192},{64,0},{128,64},{192,128},{1,193},{65,1},{129,65},{193,129... | collective-permute-start | bytes 589832 | tf_op jit(solution)/shard_map/ppermute | solution.py:29
  (9 other events, 52.8 us)
